TPU v7x, 128 devices: a whole 4x4x4 slice. The times are simulated.
128 devices in a mesh: head: 8 (over y, core), row: 16 (over x, z).
Axes of the slice: x: 4, y: 4, z: 4, core: 2. Of those that a mesh axis runs over, the one named last changes fastest.
Arguments:
- hidden_in: bfloat16 [512, 2048], replicated, may hold values from -6 to 6
- w_query: bfloat16 [2048, 16, 128], P(None, 'head', 'row'), may hold values from -0.125 to 0.125
- w_key: bfloat16 [2048, 16, 128], P(None, 'head', 'row'), may hold values from -0.125 to 0.125
- w_value: bfloat16 [2048, 32, 128], P(None, 'head'), may hold values from -0.125 to 0.125
- w_zgate: bfloat16 [2048, 32, 128], P(None, 'head'), may hold values from -0.125 to 0.125
- w_decay: bfloat16 [2048, 32], P(None, 'head'), may hold values from -0.125 to 0.125
- w_beta: bfloat16 [2048, 32], P(None, 'head'), may hold values from -0.125 to 0.125
- decay_log: float32 [32], P('head'), may hold values from -1.5 to 1.5
- dt_bias: float32 [32], P('head'), may hold values from -2 to 2
- norm_gain: float32 [128], replicated, may hold values from 0.1 to 1.9
- w_out: bfloat16 [32, 128, 2048], P('head'), may hold values from -0.09375 to 0.09375
- state: float32 [512, 32, 128, 128], P(None, 'head', 'row'), may hold values from -6 to 6
Outputs:
- layer_out: bfloat16 [512, 2048], P('row', 'head')
- new_state: float32 [512, 32, 128, 128], P(None, 'head', 'row')
All inputs are finite; a program needn't handle non-finite values.
Results may differ from a plain program's by a relative error of at most 0.005.
Values sent between devices are 32-bit elements; how exact they have to be, the bound alone decides.
No kernel may reach another device: no remote copies, remote signals or barrier semaphores. Data moves between devices by JAX's collectives and lax.ppermute only.
A program may use at most 128 MiB of HBM per device.

v0:
```python
import jax
import jax.numpy as jnp
from jax import lax
from jax.sharding import PartitionSpec as P


def split_up(value, dim, devices):
    before, after = (value.shape[:dim], value.shape[dim + 1 :])
    return jnp.moveaxis(value.reshape(*before, devices, -1, *after), dim, 0)


def summed_on_arrival(value, axis, dim):
    devices = lax.axis_size(axis)
    pieces = lax.all_to_all(split_up(value, dim, devices), axis, 0, 0, tiled=True)
    return jnp.sum(pieces, axis=0)


def local(
    hidden_in,
    w_query,
    w_key,
    w_value,
    w_zgate,
    w_decay,
    w_beta,
    decay_log,
    dt_bias,
    norm_gain,
    w_out,
    state,
):
    query = jnp.einsum("bd,dhk->bhk", hidden_in, w_query, preferred_element_type=jnp.float32)
    keys = jnp.einsum("bd,dhk->bhk", hidden_in, w_key, preferred_element_type=jnp.float32)
    values = jnp.einsum("bd,dhv->bhv", hidden_in, w_value, preferred_element_type=jnp.float32)
    decay_in = jnp.dot(hidden_in, w_decay, preferred_element_type=jnp.float32) + dt_bias
    decay = jnp.exp(-jnp.exp(decay_log) * jax.nn.softplus(decay_in))
    beta = jax.nn.sigmoid(jnp.dot(hidden_in, w_beta, preferred_element_type=jnp.float32))
    group = state.shape[1] // keys.shape[1]

    def widen(array):
        return jnp.repeat(array, group, axis=1)

    def read_state(source, vector):
        return jnp.einsum("bhkv,bhk->bhv", source, widen(vector), precision=lax.Precision.HIGHEST)

    query_sq, key_sq, raw_dot, raw_readk, raw_readq = lax.psum(
        (
            jnp.sum(query * query, axis=-1),
            jnp.sum(keys * keys, axis=-1),
            jnp.sum(query * keys, axis=-1),
            read_state(state, keys),
            read_state(state, query),
        ),
        "row",
    )
    query_scale = lax.rsqrt(1.0 + query_sq)
    key_scale = lax.rsqrt(1.0 + key_sq)
    readq_old = raw_readq * widen(query_scale)[..., None]
    unit_dot = raw_dot * query_scale * key_scale
    key_unit = keys * key_scale[..., None]
    readk = raw_readk * widen(key_scale)[..., None]
    delta = beta[..., None] * (values - decay[..., None] * readk)
    new_state = decay[..., None, None] * state + widen(key_unit)[..., None] * delta[:, :, None, :]
    own_rows = hidden_in.shape[0] // lax.axis_size("row")
    first_row = lax.axis_index("row") * own_rows
    readq_all = decay[..., None] * readq_old + widen(unit_dot)[..., None] * delta
    readq = lax.dynamic_slice_in_dim(readq_all, first_row, own_rows, 0)
    own_hidden = lax.dynamic_slice_in_dim(hidden_in, first_row, own_rows, 0)
    zgate = jnp.einsum("bd,dhv->bhv", own_hidden, w_zgate, preferred_element_type=jnp.float32)
    meansq = jnp.mean(readq * readq, axis=-1, keepdims=True)
    normed = (readq * lax.rsqrt(meansq + 0.5) * norm_gain * jax.nn.silu(zgate)).astype(jnp.bfloat16)
    partial_out = jnp.einsum("bhv,hvd->bd", normed, w_out, preferred_element_type=jnp.float32)
    layer_out = summed_on_arrival(partial_out, "head", 1).astype(jnp.bfloat16)
    return (layer_out, new_state)


def solution(mesh):
    in_specs = (
        P(),
        P(None, "head", "row"),
        P(None, "head", "row"),
        P(None, "head", None),
        P(None, "head", None),
        P(None, "head"),
        P(None, "head"),
        P("head"),
        P("head"),
        P(),
        P("head", None, None),
        P(None, "head", "row", None),
    )
    out_specs = (P("row", "head"), P(None, "head", "row", None))
    return jax.shard_map(local, mesh=mesh, in_specs=in_specs, out_specs=out_specs, check_vma=False)
```

profile of v0, /device:TPU:0, one launch (start us, length us, event | category | flops | bytes accessed | tf_op | source)
XLA Modules:
  0.0 176.4 jit_solution(13233096297192250769)
XLA Ops:
  7.2 0.0 copy-start
  7.2 0.0 copy-start.2
  7.2 0.0 all-reduce.4.cloned.1.call-start
  7.2 1.5 copy-done
  8.8 1.5 convolution_bitcast_fusion
  10.2 0.3 copy.23
  10.5 0.0 copy-done.2
  10.5 0.7 multiply_reduce_fusion.3
  11.2 0.2 copy.21
  11.4 0.4 broadcast_in_dim.15
  11.8 15.5 %fusion.45 = f32[512,4,1,128]{3,2,1,0:T(1,128)S(1)} fusion(f32[512,4,8,1]{2,3,1,0:T(1,128)S(1)} %bitcast.67, f32[512,4,8,128]{3,2,1,0:T(8,128)} %param.23), kind=kOutput, calls=%fused_computation.52 | convolution fusion | flops 25165824 | bytes 9502720 | tf_op jit(solution)/shard_map/bhkv,bhk->bhv/dot_general | solution.py:44
  27.3 0.4 broadcast_in_dim.12
  27.7 15.5 %fusion.44 = f32[512,4,1,128]{3,2,1,0:T(1,128)S(1)} fusion(f32[512,4,8,1]{2,3,1,0:T(1,128)S(1)} %bitcast.68, f32[512,4,8,128]{3,2,1,0:T(8,128)} %param.23), kind=kOutput, calls=%fused_computation.51 | convolution fusion | flops 25165824 | bytes 9502720 | tf_op jit(solution)/shard_map/bhkv,bhk->bhv/dot_general | solution.py:44
  43.2 1.5 copy_bitcast_fusion
  44.6 0.0 copy-start.7
  44.6 0.0 copy-start.3
  44.6 0.0 copy-start.6
  44.6 0.0 all-reduce.4.cloned.1.call-update
  44.6 0.0 copy-start.4
  44.7 76.2 %all-reduce = (f32[512,2]{0,1:T(2,128)S(1)}, f32[512,2]{0,1:T(2,128)S(1)}, f32[512,2]{0,1:T(2,128)S(1)}) all-reduce(f32[512,2]{0,1:T(2,128)S(1)} %get-tuple-element.4, f32[512,2]{0,1:T(2,128)S(1)} %get-tuple-element.3, f32[512,2]{0,1:T(2,128)S(1)} %get-tuple-element.2), channel_id=1, replica_groups=mesh['head'=8,'row'=16] {'row'}, use_global_device_ids=true, to_apply=%region_6.7 | all-reduce | flops 3072 | bytes 24576 | tf_op jit(solution)/shard_map/psum | solution.py:46
  120.9 0.0 copy-done.7
  121.0 0.0 copy-done.3
  121.0 0.0 copy-done.6
  121.0 0.7 fusion.39
  121.7 0.1 copy.26
  121.8 1.0 copy.27
  122.8 0.1 constant_dynamic-slice_fusion
  122.9 0.1 constant_dynamic-slice_fusion.1
  123.0 0.0 copy-done.4
  123.0 0.7 fusion.17
  123.6 15.1 %all-reduce.4.cloned.1.call-done = (f32[512,4,128]{2,0,1:T(8,128)}, f32[512,4,128]{2,0,1:T(8,128)}) async-done(((f32[512,4,128]{2,0,1:T(8,128)}, f32[512,4,128]{2,0,1:T(8,128)}), (f32[512,4,128]{2,0,1:T(8,128)}, f32[512,4,128]{2,0,1:T(8,128)})) %all-reduce.4.cloned.1.call-update) | async-done | bytes 2097168 | tf_op jit(solution)/shard_map/psum | solution.py:46
  138.8 3.1 %fusion.10 = f32[512,4,128]{2,0,1:T(8,128)S(1)} fusion(bf16[2048,4,128]{2,1,0:T(4,128)(2,1)} %param.15, bf16[512,2048]{1,0:T(8,128)(2,1)S(1)} %copy-done, f32[512,4,128]{2,0,1:T(8,128)} %get-tuple-element.8, f32[512,4]{0,1:T(4,128)S(1)} %mul.150, f32[512,4]{0,1:T(4,128)S(1)} %fusion.17, f32[512,4]{0,1:T(4,128)S(1)} %fusion.39), kind=kOutput, calls=%fused_computation.7 | convolution fusion | flops 1074790400 | bytes 6316032 | tf_op jit(solution)/shard_map/bd,dhv->bhv/dot_general | solution.py:34
  141.9 0.0 copy-start.1
  141.9 0.0 copy-start.5
  142.0 0.7 copy.28
  142.6 0.3 copy-done.1
  142.9 1.0 multiply_reduce_fusion
  144.0 0.0 copy-done.5
  144.0 3.9 %fusion.30 = f32[32,2048,1]{1,0,2:T(8,128)} fusion(bf16[4,128,2048]{2,1,0:T(8,128)(2,1)} %param.22, bf16[2048,4,128]{2,1,0:T(4,128)(2,1)} %param.16, bf16[512,2048]{1,0:T(8,128)(2,1)S(1)} %copy-done, s32[]{:T(128)S(6)} %select_n.9, f32[128]{0:T(128)S(1)} %copy-done.5, f32[32,4]{0,1:T(4,128)S(1)} %add_rsqrt_fusion.2, f32[512,4,128]{2,0,1:T(8,128)} %copy-done.1, ...), kind=kOutput, calls=%fused_computation.27 | convolution fusion | flops 134414336 | bytes 4728320 | tf_op jit(solution)/shard_map/bhv,hvd->bd/dot_general | solution.py:72
  147.9 1.7 copy.49
  149.5 4.3 %all-to-all-start = ((f32[8,32,256]{2,1,0:T(8,128)}), f32[8,32,256]{2,1,0:T(8,128)}, u32[]{:S(2)}, u32[]{:S(2)}) async-start(f32[8,32,256]{2,1,0:T(8,128)} %bitcast.70), calls=%async_computation | async-start | bytes 524288 | tf_op jit(solution)/shard_map/all_to_all | solution.py:14
  153.8 1.4 broadcast_in_dim.33
  155.2 12.7 %multiply_add_fusion = f32[512,4,8,128]{3,2,1,0:T(8,128)} fusion(f32[512,4,8,128]{3,2,1,0:T(8,128)} %param.23, f32[512,4,128]{2,1,0:T(4,128)S(1)} %copy.28, f32[512,4,8]{2,1,0:T(4,128)S(1)} %bitcast.66, f32[512,4]{1,0:T(8,128)S(1)} %copy.26), kind=kLoop, calls=%fused_computation | loop fusion | flops 6291456 | bytes 17899520 | tf_op jit(solution)/shard_map/add | solution.py:63
  167.9 0.0 all-to-all-done
  167.9 1.6 reduce_sum.49
  (10 shorter events, 0.1 us)
Async XLA Ops:
  7.2 1.6 copy-start
  7.2 3.3 %copy-start.2 = (bf16[2048,2,8]{0,2,1:T(8,128)(2,1)S(1)}, bf16[2048,2,8]{0,2,1:T(8,128)(2,1)}, u32[]{:S(2)}) copy-start(bf16[2048,2,8]{0,2,1:T(8,128)(2,1)} %param.13) | copy-start | bytes 196612
  7.2 131.6 %all-reduce.4.cloned.1.call-start = ((), (), s32[]{:S(2)}) async-start(), calls=%async_computation.1 | async-start | bytes 4194304 | tf_op jit(solution)/shard_map/psum | solution.py:46
  44.6 76.3 %copy-start.7 = (f32[4]{0:T(128)S(1)}, f32[4]{0:T(128)}, u32[]{:S(2)}) copy-start(f32[4]{0:T(128)} %param.19) | copy-start | bytes 52
  44.6 76.3 %copy-start.3 = (bf16[2048,4]{0,1:T(4,128)(2,1)S(1)}, bf16[2048,4]{0,1:T(4,128)(2,1)}, u32[]{:S(2)}) copy-start(bf16[2048,4]{0,1:T(4,128)(2,1)} %param.17) | copy-start | bytes 49156
  44.6 76.3 %copy-start.6 = (f32[4]{0:T(128)S(1)}, f32[4]{0:T(128)}, u32[]{:S(2)}) copy-start(f32[4]{0:T(128)} %param.20) | copy-start | bytes 52
  44.6 78.3 %copy-start.4 = (bf16[2048,4]{0,1:T(4,128)(2,1)S(1)}, bf16[2048,4]{0,1:T(4,128)(2,1)}, u32[]{:S(2)}) copy-start(bf16[2048,4]{0,1:T(4,128)(2,1)} %param.18) | copy-start | bytes 49156
  141.9 1.0 copy-start.1
  141.9 2.0 %copy-start.5 = (f32[128]{0:T(128)S(1)}, f32[128]{0:T(128)}, u32[]{:S(2)}) copy-start(f32[128]{0:T(128)} %param.21) | copy-start | bytes 1540
  149.5 18.4 %all-to-all-start = ((f32[8,32,256]{2,1,0:T(8,128)}), f32[8,32,256]{2,1,0:T(8,128)}, u32[]{:S(2)}, u32[]{:S(2)}) async-start(f32[8,32,256]{2,1,0:T(8,128)} %bitcast.70), calls=%async_computation | async-start | bytes 524288 | tf_op jit(solution)/shard_map/all_to_all | solution.py:14
Sparse Core Ops, SparseCore 0:
  44.8 93.9 all-reduce.3
where the time goes:
time: 178 us; the launch traced here: 176 us
  blocking collectives  76.2 us (43%)
  matrix products  41.5 us (23%)
  other arithmetic  15.4 us (9%)
  waiting for transfers between devices  15.2 us (9%)
  between operations  14.3 us (8%)
  local copies, waits for them, and re-layouts  9.59 us (5%)
  starting transfers between devices  4.33 us (2%)
    psum x1, blocking collectives, local(): lax.psum((jnp.sum(query * query, axis=-1), jnp.sum(keys * keys, axis=-1),...  76.2 us
    dot_general x2, matrix products, read_state(): jnp.einsum('bhkv,bhk->bhv', source, widen(vector), precision=lax.Precisio...  31 us
    psum x1, waiting for transfers between devices, local(): lax.psum((jnp.sum(query * query, axis=-1), jnp.sum(keys * keys, axis=-1),...  15.1 us
    add x1, other arithmetic, local(): decay[..., None, None] * state  12.7 us
    all_to_all x1, starting transfers between devices, summed_on_arrival(): lax.all_to_all(split_up(value, dim, devices), axis, 0, 0, tiled=True)  4.29 us
    dot_general x1, matrix products, local(): jnp.einsum('bhv,hvd->bd', normed, w_out, preferred_element_type=jnp.float32)  3.91 us
  transfers between devices with their start and end apart: 2, of which 1 were waited for; matrix products, arithmetic and copies ran while one was open for 10% of the time, Pallas kernels for 0%

commit v1 on v0

v1 whole, which is shorter than its diff:
```python
import jax
import jax.numpy as jnp
from jax import lax
from jax.experimental import pallas as pl
from jax.experimental.pallas import tpu as pltpu
from jax.sharding import PartitionSpec as P

LANES = 128
SUB = 8


def spread(column):
    return jnp.broadcast_to(column, (SUB, LANES))


def rows_summed(tiles, row):
    step = 1
    while len(tiles) > 1:
        keep = (row & step) != 0
        merged = []
        for low, high in zip(tiles[0::2], tiles[1::2]):
            merged.append(jnp.where(keep, high, low) + pltpu.roll(jnp.where(keep, low, high), step, 0))
        tiles = merged
        step *= 2
    return tiles[0]


def own_lanes(ref, part, rows):
    per_tile = LANES // rows
    tile = ref[:, pl.ds(pl.multiple_of(part // per_tile * LANES, LANES), LANES)]
    shift = (LANES - part % per_tile * rows) % LANES
    return pltpu.roll(tile, shift, 1)


def read_kernel(hidden, w_query, w_key, w_decay, decay_log, dt_bias, state, sent, keys_out, decay_out, weights, vectors, sums):
    part = pl.program_id(0)
    key_rows = w_query.shape[0]
    heads = w_decay.shape[0]
    seqs = hidden.shape[0]
    rows = state.shape[0]
    key_heads = key_rows // SUB
    group = heads // key_heads

    @pl.when(part == 0)
    def _():
        weights[...] = jnp.zeros(weights.shape, weights.dtype)
        weights[0:key_rows] = w_query[...]
        weights[key_rows : 2 * key_rows] = w_key[...]
        weights[2 * key_rows : 2 * key_rows + heads] = w_decay[...]
        projected = lax.dot_general(weights[...], hidden[...], (((1,), (1,)), ((), ())), preferred_element_type=jnp.float32)
        query = projected[0:key_rows]
        keys = projected[key_rows : 2 * key_rows]
        vectors[...] = projected[0 : 2 * key_rows]
        keys_out[...] = keys
        pre = projected[2 * key_rows : 2 * key_rows + heads] + dt_bias[...]
        soft = jnp.maximum(pre, 0.0) + jnp.log1p(jnp.exp(-jnp.abs(pre)))
        decay = jnp.exp(-jnp.exp(decay_log[...]) * soft)
        for h in range(heads):
            decay_out[h * SUB : (h + 1) * SUB] = jnp.broadcast_to(decay[h : h + 1], (SUB, seqs))
        sums[...] = jnp.zeros(sums.shape, sums.dtype)
        for n, product in enumerate((query * query, keys * keys, query * keys)):
            for g in range(key_heads):
                sums[n * key_heads + g : n * key_heads + g + 1] = jnp.sum(product[g * SUB : (g + 1) * SUB], axis=0, keepdims=True)

    row = lax.broadcasted_iota(jnp.int32, (SUB, LANES), 0)
    mine = own_lanes(vectors, part, rows)
    for first in range(0, rows, SUB):
        for g in range(key_heads):
            by_key = [[] for _ in range(group)]
            by_query = [[] for _ in range(group)]
            for b in range(first, first + SUB):
                q = spread(mine[g * SUB : (g + 1) * SUB, b : b + 1])
                k = spread(mine[key_rows + g * SUB : key_rows + (g + 1) * SUB, b : b + 1])
                for j in range(group):
                    tile = state[b, g * group + j]
                    by_key[j].append(tile * k)
                    by_query[j].append(tile * q)
            for j in range(group):
                h = g * group + j
                sent[0, h * rows + first : h * rows + first + SUB] = rows_summed(by_key[j], row)
                at = (heads + h) * rows + first
                sent[0, at : at + SUB] = rows_summed(by_query[j], row)
    sent[0, 2 * heads * rows : 2 * heads * rows + SUB] = own_lanes(sums, part, rows)


def owner_kernel(arrived, values, zgate, decay, beta, norm_gain, delta_out, normed_out):
    rows, heads = decay.shape
    key_heads = 2
    group = heads // key_heads
    total = arrived[0]
    for n in range(1, arrived.shape[0]):
        total = total + arrived[n]
    sums = jnp.transpose(total[2 * heads * rows :])[0:rows]
    query_scale = lax.rsqrt(1.0 + sums[:, 0:key_heads])
    key_scale = lax.rsqrt(1.0 + sums[:, key_heads : 2 * key_heads])
    unit_dot = sums[:, 2 * key_heads : 3 * key_heads] * query_scale * key_scale
    for h in range(heads):
        g = h // group
        lanes = slice(h * LANES, (h + 1) * LANES)
        d = decay[:, h : h + 1]
        ks = key_scale[:, g : g + 1]
        readk = total[h * rows : (h + 1) * rows] * ks
        delta = beta[:, h : h + 1] * (values[:, lanes] - d * readk)
        raw_q = total[(heads + h) * rows : (heads + h + 1) * rows]
        readq = d * (raw_q * query_scale[:, g : g + 1]) + unit_dot[:, g : g + 1] * delta
        meansq = jnp.mean(readq * readq, axis=1, keepdims=True)
        z = zgate[:, lanes]
        normed = readq * lax.rsqrt(meansq + 0.5) * norm_gain[...] * (z / (1.0 + jnp.exp(-z)))
        normed_out[:, lanes] = normed.astype(jnp.bfloat16)
        scaled = delta * ks
        for n in range(delta_out.shape[0]):
            delta_out[n, h * rows : (h + 1) * rows] = scaled


def update_kernel(keys, decay, delta, state, new_state):
    part = pl.program_id(0)
    rows, heads = state.shape[0:2]
    key_heads = keys.shape[0] // SUB
    group = heads // key_heads
    my_keys = own_lanes(keys, part, rows)
    my_decay = own_lanes(decay, part, rows)
    for b in range(rows):
        for g in range(key_heads):
            k = spread(my_keys[g * SUB : (g + 1) * SUB, b : b + 1])
            for h in range(g * group, (g + 1) * group):
                d = spread(my_decay[h * SUB : (h + 1) * SUB, b : b + 1])
                row = jnp.broadcast_to(delta[0, h * rows + b : h * rows + b + 1], (SUB, LANES))
                new_state[b, h] = d * state[b, h] + k * row


def local(
    hidden_in,
    w_query,
    w_key,
    w_value,
    w_zgate,
    w_decay,
    w_beta,
    decay_log,
    dt_bias,
    norm_gain,
    w_out,
    state,
):
    parts = lax.axis_size("row")
    seqs, width = hidden_in.shape
    rows = seqs // parts
    heads = state.shape[1]
    key_rows = w_query.shape[1] * w_query.shape[2]
    per_part = 2 * heads * rows + SUB
    f32 = jnp.float32

    def whole(*shape):
        return pl.BlockSpec(shape, lambda n: (0,) * len(shape))

    state_block = pl.BlockSpec((rows, heads, SUB, LANES), lambda n: (n, 0, 0, 0))
    limit = pltpu.CompilerParams(vmem_limit_bytes=24 * 1024 * 1024)
    sent, keys, decay_wide = pl.pallas_call(
        read_kernel,
        grid=(parts,),
        in_specs=[
            whole(seqs, width),
            whole(key_rows, width),
            whole(key_rows, width),
            whole(heads, width),
            whole(heads, 1),
            whole(heads, 1),
            state_block,
        ],
        out_specs=[
            pl.BlockSpec((1, per_part, LANES), lambda n: (n, 0, 0)),
            whole(key_rows, seqs),
            whole(heads * SUB, seqs),
        ],
        out_shape=[
            jax.ShapeDtypeStruct((parts, per_part, LANES), f32),
            jax.ShapeDtypeStruct((key_rows, seqs), f32),
            jax.ShapeDtypeStruct((heads * SUB, seqs), f32),
        ],
        scratch_shapes=[
            pltpu.VMEM((2 * key_rows + 16, width), jnp.bfloat16),
            pltpu.VMEM((2 * key_rows, seqs), f32),
            pltpu.VMEM((SUB, seqs), f32),
        ],
        compiler_params=limit,
        name="read_state",
    )(
        hidden_in,
        jnp.transpose(w_query, (1, 2, 0)).reshape(key_rows, width),
        jnp.transpose(w_key, (1, 2, 0)).reshape(key_rows, width),
        jnp.transpose(w_decay),
        decay_log[:, None],
        dt_bias[:, None],
        state,
    )
    arrived = lax.all_to_all(sent, "row", 0, 0, tiled=True)

    own_hidden = lax.dynamic_slice_in_dim(hidden_in, lax.axis_index("row") * rows, rows, 0)
    values = jnp.einsum("bd,dhv->bhv", own_hidden, w_value, preferred_element_type=f32).reshape(rows, heads * LANES)
    zgate = jnp.einsum("bd,dhv->bhv", own_hidden, w_zgate, preferred_element_type=f32).reshape(rows, heads * LANES)
    decay_in = jnp.dot(own_hidden, w_decay, preferred_element_type=f32) + dt_bias
    decay = jnp.exp(-jnp.exp(decay_log) * jax.nn.softplus(decay_in))
    beta = jax.nn.sigmoid(jnp.dot(own_hidden, w_beta, preferred_element_type=f32))

    delta_own, normed = pl.pallas_call(
        owner_kernel,
        out_shape=[
            jax.ShapeDtypeStruct((parts, heads * rows, LANES), f32),
            jax.ShapeDtypeStruct((rows, heads * LANES), jnp.bfloat16),
        ],
        compiler_params=limit,
        name="owner_rows",
    )(arrived, values, zgate, decay, beta, norm_gain[None])
    delta = lax.all_to_all(delta_own, "row", 0, 0, tiled=True)

    partial_out = jnp.dot(normed, w_out.reshape(heads * LANES, -1), preferred_element_type=f32)
    tall = lax.axis_size("head")
    pieces = jnp.moveaxis(partial_out.reshape(rows, tall, -1), 1, 0)
    pieces = lax.all_to_all(pieces, "head", 0, 0, tiled=True)
    layer_out = jnp.sum(pieces, axis=0).astype(jnp.bfloat16)

    new_state = pl.pallas_call(
        update_kernel,
        grid=(parts,),
        in_specs=[
            whole(key_rows, seqs),
            whole(heads * SUB, seqs),
            pl.BlockSpec((1, heads * rows, LANES), lambda n: (n, 0, 0)),
            state_block,
        ],
        out_specs=state_block,
        out_shape=jax.ShapeDtypeStruct(state.shape, f32),
        compiler_params=limit,
        name="update_state",
    )(keys, decay_wide, delta, state)
    return (layer_out, new_state)


def solution(mesh):
    in_specs = (
        P(),
        P(None, "head", "row"),
        P(None, "head", "row"),
        P(None, "head", None),
        P(None, "head", None),
        P(None, "head"),
        P(None, "head"),
        P("head"),
        P("head"),
        P(),
        P("head", None, None),
        P(None, "head", "row", None),
    )
    out_specs = (P("row", "head"), P(None, "head", "row", None))
    return jax.shard_map(local, mesh=mesh, in_specs=in_specs, out_specs=out_specs, check_vma=False)
```

time: 178 us -> 107 us (0.60)
  blocking collectives: 76.2 us -> 11.8 us
  matrix products: 41.5 us -> 5.76 us
  waiting for transfers between devices: 15.2 us -> 39 us
  Pallas kernels: 0 us -> 18.8 us
  other arithmetic: 15.4 us -> 0.63 us
  between operations: 14.3 us -> 0.79 us
  local copies, waits for them, and re-layouts: 9.59 us -> 17.8 us
  starting transfers between devices: 4.33 us -> 11.7 us
    psum x1 -> x0, blocking collectives: 76.2 us -> none  [local(): lax.psum((jnp.sum(query * query, axis=-1), jnp.sum(keys * keys, axis=-1),...]
    all_to_all x1 -> x2, waiting for transfers between devices: 0.01 us -> 39 us  [the longest x1 22.1 us: local(): arrived = lax.all_to_all(sent, 'row', 0, 0, tiled=True)]
    dot_general x6 -> x5, matrix products: 39.4 us -> 5.76 us  [the longest x1 1.51 us: local(): jnp.einsum('bd,dhv->bhv', own_hidden, w_value, preferred_element_type=f32)]
    pallas_call x0 -> x3, Pallas kernels: none -> 18.8 us  [the longest x1 9.88 us: local(): pl.pallas_call(update_kernel, grid=(parts,), in_specs=[whole(key_rows, se...]
    psum x1 -> x0, waiting for transfers between devices: 15.1 us -> none  [local(): lax.psum((jnp.sum(query * query, axis=-1), jnp.sum(keys * keys, axis=-1),...]
    add x1 -> x0, other arithmetic: 12.7 us -> none  [local(): decay[..., None, None] * state]
    all_to_all x0 -> x1, blocking collectives: none -> 11.8 us  [local(): pieces = lax.all_to_all(pieces, 'head', 0, 0, tiled=True)]
    unnamed x16 -> x32, local copies, waits for them, and re-layouts: 1.83 us -> 12.3 us
  transfers between devices with their start and end apart: 2 -> 2, of which waited for: 1 -> 2; matrix products, arithmetic and copies ran while one was open for 10% -> 9% of each run, Pallas kernels for 0% -> 0%
where the time goes in v1:
time: 107 us; the launch traced here: 106 us
  waiting for transfers between devices  39 us (36%)
  Pallas kernels  18.8 us (18%)
  local copies, waits for them, and re-layouts  17.8 us (17%)
  blocking collectives  11.8 us (11%)
  starting transfers between devices  11.7 us (11%)
  matrix products  5.76 us (5%)
    all_to_all x1, waiting for transfers between devices, local(): arrived = lax.all_to_all(sent, 'row', 0, 0, tiled=True)  22.1 us
    all_to_all x1, waiting for transfers between devices, local(): delta = lax.all_to_all(delta_own, 'row', 0, 0, tiled=True)  16.9 us
    unnamed x32, local copies, waits for them, and re-layouts  12.3 us
    all_to_all x1, blocking collectives, local(): pieces = lax.all_to_all(pieces, 'head', 0, 0, tiled=True)  11.8 us
    pallas_call x1, Pallas kernels, local(): pl.pallas_call(update_kernel, grid=(parts,), in_specs=[whole(key_rows, se...  9.88 us
    all_to_all x1, starting transfers between devices, local(): arrived = lax.all_to_all(sent, 'row', 0, 0, tiled=True)  8.03 us
    pallas_call x1, Pallas kernels, local(): pl.pallas_call(read_kernel, grid=(parts,), in_specs=[whole(seqs, width),...  6.76 us
    dot_general x1, local copies, waits for them, and re-layouts, local(): jnp.dot(normed, w_out.reshape(heads * LANES, -1), preferred_element_type=...  3.92 us
  transfers between devices with their start and end apart: 2, of which 2 were waited for; matrix products, arithmetic and copies ran while one was open for 9% of the time, Pallas kernels for 0%

profile of v1, /device:TPU:0, one launch (start us, length us, event | category | flops | bytes accessed | tf_op | source)
XLA Modules:
  0.0 106.3 jit_solution(8612624634258687024)
XLA Ops:
  0.6 0.0 copy-start
  0.6 0.9 copy.24.dt_bias
  1.5 0.7 copy.23.decay_log
  2.3 0.0 copy-start.1
  2.3 3.4 %copy-done.1 = f32[512,4,8,128]{3,2,1,0:T(8,128)S(1)} copy-done((f32[512,4,8,128]{3,2,1,0:T(8,128)S(1)}, f32[512,4,8,128]{3,2,1,0:T(8,128)}, u32[]{:S(2)}) %copy-start.1) | copy-done | bytes 8388632
  5.7 0.0 copy-start.4
  5.7 1.6 %copy-done.4 = bf16[512,2048]{1,0:T(8,128)(2,1)S(1)} copy-done((bf16[512,2048]{1,0:T(8,128)(2,1)S(1)}, bf16[512,2048]{1,0:T(8,128)(2,1)}, u32[]{:S(2)}) %copy-start.4) | copy-done | bytes 2097176
  7.3 0.0 copy-start.6
  7.3 0.8 copy-done.6
  8.1 0.0 copy-start.7
  8.1 0.8 copy-done.7
  8.9 0.0 copy-start.8
  8.9 0.7 copy-done.8
  9.6 6.8 %read_state.1 = (f32[16,264,128]{2,1,0:T(8,128)S(1)}, f32[16,512]{1,0:T(8,128)S(1)}, f32[32,512]{1,0:T(8,128)S(1)}) custom-call(bf16[512,2048]{1,0:T(8,128)(2,1)S(1)} %copy-done.4, bf16[16,2048]{1,0:T(8,128)(2,1)S(1)} %bitcast.35, bf16[16,2048]{1,0:T(8,128)(2,1)S(1)} %bitcast.36, bf16[4,2048]{1,0:T(4,128)(2,1)S(1)} %bitcast.37, f32[4,1]{1,0:T(4,128)S(1)} %copy.23.decay_log, ...), custom_call_target="tpu_custom_call" | custom-call | tf_op jit(solution)/shard_map/read_state/pallas_call | solution.py:158
  16.4 0.0 copy-start.3
  16.4 1.3 %copy-done.3 = f32[16,264,128]{2,1,0:T(8,128)} copy-done((f32[16,264,128]{2,1,0:T(8,128)}, f32[16,264,128]{2,1,0:T(8,128)S(1)}, u32[]{:S(2)}) %copy-start.3) | copy-done | bytes 2162712
  17.8 8.0 %all-to-all-start = ((f32[16,264,128]{2,1,0:T(8,128)}), f32[16,264,128]{2,1,0:T(8,128)}, u32[]{:S(2)}, u32[]{:S(2)}) async-start(f32[16,264,128]{2,1,0:T(8,128)} %copy-done.3), calls=%async_computation | async-start | bytes 4325376 | tf_op jit(solution)/shard_map/all_to_all | solution.py:196
  25.8 3.9 %copy.34 = bf16[2048,512]{1,0:T(8,128)(2,1)} copy(bf16[2048,512]{0,1:T(8,128)(2,1)} %bitcast.40) | data formatting | bytes 4194304 | tf_op jit(solution)/shard_map/dot_general | solution.py:216
  29.7 0.0 copy-done
  29.7 0.0 copy-start.14
  29.7 0.0 copy-start.12
  29.7 0.0 copy-start.15
  29.8 0.0 copy-start.9
  29.8 0.0 copy-start.13
  29.8 0.0 copy-start.10
  29.8 1.5 %fusion.4 = f32[4,4,8,128]{3,2,1,0:T(8,128)S(1)} fusion(bf16[2048,4,128]{2,1,0:T(4,128)(2,1)S(1)} %copy-done, bf16[512,2048]{1,0:T(8,128)(2,1)} %hidden.1, s32[]{:T(128)S(6)} %select_n.7), kind=kOutput, calls=%fused_computation.5 | convolution fusion | flops 67108864 | bytes 2293764 | tf_op jit(solution)/shard_map/bd,dhv->bhv/dot_general | solution.py:199
  31.3 0.1 copy-done.14
  31.4 1.4 %fusion.7 = f32[4,4,8,128]{3,2,1,0:T(8,128)S(1)} fusion(bf16[2048,4,128]{2,1,0:T(4,128)(2,1)S(1)} %copy-done.14, bf16[512,2048]{1,0:T(8,128)(2,1)} %hidden.1, s32[]{:T(128)S(6)} %select_n.7), kind=kOutput, calls=%fused_computation.6 | convolution fusion | flops 67108864 | bytes 2293764 | tf_op jit(solution)/shard_map/bd,dhv->bhv/dot_general | solution.py:200
  32.8 0.0 copy-done.12
  32.8 0.0 copy-done.15
  32.8 1.1 %fusion.12.beta = f32[32,4]{1,0:T(8,128)S(1)} fusion(bf16[2048,4]{0,1:T(4,128)(2,1)S(1)} %copy-done.15, bf16[512,2048]{1,0:T(8,128)(2,1)} %hidden.1, s32[]{:T(128)S(6)} %select_n.7), kind=kOutput, calls=%fused_computation.10 | convolution fusion | flops 524672 | bytes 147972 | tf_op jit(solution)/shard_map/dot_general | solution.py:203
  33.9 0.0 copy-done.9
  33.9 0.0 copy-done.13
  33.9 1.1 %fusion.21.decay = f32[32,4]{1,0:T(8,128)S(1)} fusion(bf16[2048,4]{0,1:T(4,128)(2,1)S(1)} %copy-done.9, bf16[512,2048]{1,0:T(8,128)(2,1)} %hidden.1, s32[]{:T(128)S(6)} %select_n.7, f32[4]{0:T(128)S(1)} %copy-done.13, f32[4]{0:T(128)S(1)} %exponential_negate_fusion), kind=kOutput, calls=%fused_computation.23 | convolution fusion | flops 525312 | bytes 148004 | tf_op jit(solution)/shard_map/dot_general | solution.py:201
  35.0 22.1 %all-to-all-done.arrived = f32[16,264,128]{2,1,0:T(8,128)} async-done(((f32[16,264,128]{2,1,0:T(8,128)}), f32[16,264,128]{2,1,0:T(8,128)}, u32[]{:S(2)}, u32[]{:S(2)}) %all-to-all-start) | async-done | bytes 2162720 | tf_op jit(solution)/shard_map/all_to_all | solution.py:196
  57.1 0.0 copy-start.11
  57.1 0.0 copy-done.10
  57.1 2.2 %owner_rows.1 = (f32[16,128,128]{2,1,0:T(8,128)S(1)}, bf16[32,512]{1,0:T(8,128)(2,1)S(1)}) custom-call(f32[16,264,128]{2,1,0:T(8,128)} %all-to-all-done.arrived, f32[32,512]{1,0:T(8,128)S(1)} %get-tuple-element.13.values, f32[32,512]{1,0:T(8,128)S(1)} %get-tuple-element.12.zgate, f32[32,4]{1,0:T(8,128)S(1)} %fusion.21.decay, f32[32,4]{1,0:T(8,128)S(1)} %fusion.12.beta, ...), custom_call_target="tpu_custom_call" | custom-call | tf_op jit(solution)/shard_map/owner_rows/pallas_call | solution.py:205
  59.3 0.0 copy-start.5
  59.3 0.0 copy-done.11
  59.3 0.7 convolution_bitcast_fusion
  60.0 11.8 %all_to_all.15 = f32[8,32,256]{2,1,0:T(8,128)S(1)} all-to-all(f32[8,32,256]{2,1,0:T(8,128)S(1)} %convolution_bitcast_fusion), channel_id=1, replica_groups=mesh['head'=8,'row'=16] {'head'}, dimensions={0} | all-to-all | bytes 524288 | tf_op jit(solution)/shard_map/all_to_all | solution.py:219
  71.8 0.0 copy-done.5
  71.8 3.7 %all-to-all-start.2 = ((f32[16,128,128]{2,1,0:T(8,128)}), f32[16,128,128]{2,1,0:T(8,128)S(1)}, u32[]{:S(2)}, u32[]{:S(2)}) async-start(f32[16,128,128]{2,1,0:T(8,128)} %copy-done.5), calls=%async_computation.2 | async-start | bytes 2097152 | tf_op jit(solution)/shard_map/all_to_all | solution.py:214
  75.5 0.6 reduce_sum.9
  76.1 16.9 %all-to-all-done.2.delta = f32[16,128,128]{2,1,0:T(8,128)S(1)} async-done(((f32[16,128,128]{2,1,0:T(8,128)}), f32[16,128,128]{2,1,0:T(8,128)S(1)}, u32[]{:S(2)}, u32[]{:S(2)}) %all-to-all-start.2) | async-done | bytes 1048608 | tf_op jit(solution)/shard_map/all_to_all | solution.py:214
  93.0 0.0 copy-start.2
  93.1 3.4 %copy-done.2 = f32[512,4,8,128]{3,2,1,0:T(8,128)S(1)} copy-done((f32[512,4,8,128]{3,2,1,0:T(8,128)S(1)}, f32[512,4,8,128]{3,2,1,0:T(8,128)}, u32[]{:S(2)}) %copy-start.2) | copy-done | bytes 8388632
  96.4 9.9 %update_state.1 = f32[512,4,8,128]{3,2,1,0:T(8,128)} custom-call(f32[16,512]{1,0:T(8,128)S(1)} %get-tuple-element.9.keys, f32[32,512]{1,0:T(8,128)S(1)} %get-tuple-element.10.decay, f32[16,128,128]{2,1,0:T(8,128)S(1)} %all-to-all-done.2.delta, f32[512,4,8,128]{3,2,1,0:T(8,128)S(1)} %copy-done.2), custom_call_target="tpu_custom_call" | custom-call | tf_op jit(solution)/shard_map/update_state/pallas_call | solution.py:222
  (2 shorter events, 0.0 us)
Async XLA Ops:
  0.6 29.1 %copy-start = (bf16[2048,4,128]{2,1,0:T(4,128)(2,1)S(1)}, bf16[2048,4,128]{2,1,0:T(4,128)(2,1)}, u32[]{:S(2)}) copy-start(bf16[2048,4,128]{2,1,0:T(4,128)(2,1)} %param.15) | copy-start | bytes 6291460
  2.3 3.4 %copy-start.1 = (f32[512,4,8,128]{3,2,1,0:T(8,128)S(1)}, f32[512,4,8,128]{3,2,1,0:T(8,128)}, u32[]{:S(2)}) copy-start(f32[512,4,8,128]{3,2,1,0:T(8,128)} %state.3) | copy-start | bytes 25165828
  5.7 1.6 %copy-start.4 = (bf16[512,2048]{1,0:T(8,128)(2,1)S(1)}, bf16[512,2048]{1,0:T(8,128)(2,1)}, u32[]{:S(2)}) copy-start(bf16[512,2048]{1,0:T(8,128)(2,1)} %hidden.1) | copy-start | bytes 6291460
  7.3 0.8 copy-start.6
  8.1 0.8 copy-start.7
  8.9 0.7 copy-start.8
  16.4 1.3 %copy-start.3 = (f32[16,264,128]{2,1,0:T(8,128)}, f32[16,264,128]{2,1,0:T(8,128)S(1)}, u32[]{:S(2)}) copy-start(f32[16,264,128]{2,1,0:T(8,128)S(1)} %get-tuple-element.7) | copy-start | bytes 6488068
  17.8 39.3 %all-to-all-start = ((f32[16,264,128]{2,1,0:T(8,128)}), f32[16,264,128]{2,1,0:T(8,128)}, u32[]{:S(2)}, u32[]{:S(2)}) async-start(f32[16,264,128]{2,1,0:T(8,128)} %copy-done.3), calls=%async_computation | async-start | bytes 4325376 | tf_op jit(solution)/shard_map/all_to_all | solution.py:196
  29.7 1.7 %copy-start.14 = (bf16[2048,4,128]{2,1,0:T(4,128)(2,1)S(1)}, bf16[2048,4,128]{2,1,0:T(4,128)(2,1)}, u32[]{:S(2)}) copy-start(bf16[2048,4,128]{2,1,0:T(4,128)(2,1)} %param.16) | copy-start | bytes 6291460
  29.7 3.0 %copy-start.12 = (f32[4]{0:T(128)S(1)}, f32[4]{0:T(128)}, u32[]{:S(2)}) copy-start(f32[4]{0:T(128)} %param.19) | copy-start | bytes 52
  29.7 3.0 %copy-start.15 = (bf16[2048,4]{0,1:T(4,128)(2,1)S(1)}, bf16[2048,4]{0,1:T(4,128)(2,1)}, u32[]{:S(2)}) copy-start(bf16[2048,4]{0,1:T(4,128)(2,1)} %param.18) | copy-start | bytes 49156
  29.8 4.1 %copy-start.9 = (bf16[2048,4]{0,1:T(4,128)(2,1)S(1)}, bf16[2048,4]{0,1:T(4,128)(2,1)}, u32[]{:S(2)}) copy-start(bf16[2048,4]{0,1:T(4,128)(2,1)} %param.17) | copy-start | bytes 49156
  29.8 4.1 %copy-start.13 = (f32[4]{0:T(128)S(1)}, f32[4]{0:T(128)}, u32[]{:S(2)}) copy-start(f32[4]{0:T(128)} %param.20) | copy-start | bytes 52
  29.8 27.3 %copy-start.10 = (f32[128]{0:T(128)S(1)}, f32[128]{0:T(128)}, u32[]{:S(2)}) copy-start(f32[128]{0:T(128)} %param.21) | copy-start | bytes 1540
  57.1 2.2 %copy-start.11 = (bf16[2048,512]{1,0:T(8,128)(2,1)S(1)}, bf16[2048,512]{1,0:T(8,128)(2,1)}, u32[]{:S(2)}) copy-start(bf16[2048,512]{1,0:T(8,128)(2,1)} %copy.34) | copy-start | bytes 6291460
  59.3 12.5 %copy-start.5 = (f32[16,128,128]{2,1,0:T(8,128)}, f32[16,128,128]{2,1,0:T(8,128)S(1)}, u32[]{:S(2)}) copy-start(f32[16,128,128]{2,1,0:T(8,128)S(1)} %get-tuple-element.11) | copy-start | bytes 3145732
  71.8 21.2 %all-to-all-start.2 = ((f32[16,128,128]{2,1,0:T(8,128)}), f32[16,128,128]{2,1,0:T(8,128)S(1)}, u32[]{:S(2)}, u32[]{:S(2)}) async-start(f32[16,128,128]{2,1,0:T(8,128)} %copy-done.5), calls=%async_computation.2 | async-start | bytes 2097152 | tf_op jit(solution)/shard_map/all_to_all | solution.py:214
  93.0 3.4 %copy-start.2 = (f32[512,4,8,128]{3,2,1,0:T(8,128)S(1)}, f32[512,4,8,128]{3,2,1,0:T(8,128)}, u32[]{:S(2)}) copy-start(f32[512,4,8,128]{3,2,1,0:T(8,128)} %state.3) | copy-start | bytes 25165828

commit v2 on v1

v2 whole, which is shorter than its diff:
```python
import jax
import jax.numpy as jnp
from jax import lax
from jax.experimental import pallas as pl
from jax.experimental.pallas import tpu as pltpu
from jax.sharding import PartitionSpec as P


LANES = 128
SUB = 8


def high_low(value):
    high = value.astype(jnp.bfloat16)
    return high, (value - high.astype(jnp.float32)).astype(jnp.bfloat16)


def dot(left, right):
    return jnp.dot(left, right, preferred_element_type=jnp.float32)


def own_lanes(ref, part, rows):
    per_tile = LANES // rows
    tile = ref[:, pl.ds(pl.multiple_of(part // per_tile * LANES, LANES), LANES)]
    shift = (LANES - part % per_tile * rows) % LANES
    return pltpu.roll(tile, shift, 1)


def read_kernel(
    hidden_hbm,
    w_query_hbm,
    w_key_hbm,
    w_decay_hbm,
    decay_log_hbm,
    dt_bias_hbm,
    state_hbm,
    sent_hbm,
    keys_out,
    decay_out,
    hidden,
    weights,
    w_decay,
    decay_log,
    dt_bias,
    state,
    sent,
    picks_high,
    picks_low,
    sums,
    in_sems,
    state_sems,
    sent_sems,
):
    parts, rows, heads = state.shape[0:3]
    key_rows = w_query_hbm.shape[0]
    key_heads = key_rows // SUB
    group = heads // key_heads
    span = rows * SUB
    pad = weights.dtype.itemsize * SUB

    inputs = [
        pltpu.make_async_copy(hidden_hbm, hidden, in_sems.at[0]),
        pltpu.make_async_copy(w_query_hbm, weights.at[pad : pad + key_rows], in_sems.at[1]),
        pltpu.make_async_copy(w_key_hbm, weights.at[pad + key_rows : pad + 2 * key_rows], in_sems.at[2]),
        pltpu.make_async_copy(w_decay_hbm, w_decay, in_sems.at[3]),
        pltpu.make_async_copy(decay_log_hbm, decay_log, in_sems.at[4]),
        pltpu.make_async_copy(dt_bias_hbm, dt_bias, in_sems.at[5]),
    ]
    for copy in inputs:
        copy.start()

    def state_copy(n):
        return pltpu.make_async_copy(state_hbm.at[pl.ds(n * rows, rows)], state.at[n], state_sems.at[n])

    def sent_copy(n):
        return pltpu.make_async_copy(sent.at[n], sent_hbm.at[n], sent_sems.at[n])

    for n in range(parts):
        state_copy(n).start()
    width = weights.shape[1]
    weights[0:pad] = jnp.zeros((pad, width), weights.dtype)
    weights[pad + 2 * key_rows :] = jnp.zeros((LANES - pad - 2 * key_rows, width), weights.dtype)
    for copy in inputs:
        copy.wait()
    weights[0:heads] = w_decay[...]
    projected = lax.dot_general(hidden[...], weights[...], (((1,), (1,)), ((), ())), preferred_element_type=jnp.float32)
    high, low = high_low(projected)
    source = lax.broadcasted_iota(jnp.int32, (LANES, span), 0)
    entry = lax.broadcasted_iota(jnp.int32, (LANES, span), 1) % SUB
    own = lax.broadcasted_iota(jnp.int32, (rows, span), 1) // SUB == lax.broadcasted_iota(jnp.int32, (rows, span), 0)
    for kind in range(2):
        for g in range(key_heads):
            pick = (source == pad + kind * key_rows + g * SUB + entry).astype(jnp.bfloat16)
            for half, picks in ((high, picks_high), (low, picks_low)):
                wide = dot(half, pick).reshape(parts, rows, span)
                picks[:, g, kind * rows : (kind + 1) * rows] = jnp.where(own[None], wide, 0.0).astype(jnp.bfloat16)

    pre = projected[:, 0:heads] + dt_bias[...]
    soft = jnp.maximum(pre, 0.0) + jnp.log1p(jnp.exp(-jnp.abs(pre)))
    decay_out[...] = jnp.exp(-jnp.exp(decay_log[...]) * soft)

    turned = jnp.transpose(projected)
    query = turned[pad : pad + key_rows]
    keys = turned[pad + key_rows : pad + 2 * key_rows]
    keys_out[...] = keys
    sums[...] = jnp.zeros(sums.shape, sums.dtype)
    for n, product in enumerate((query * query, keys * keys, query * keys)):
        for g in range(key_heads):
            sums[n * key_heads + g : n * key_heads + g + 1] = jnp.sum(product[g * SUB : (g + 1) * SUB], axis=0, keepdims=True)

    @pl.loop(0, parts)
    def _(part):
        state_copy(part).wait()
        for g in range(key_heads):
            tiles = [state[part, :, g * group + j].reshape(span, LANES) for j in range(group)]
            state_high, state_low = high_low(jnp.concatenate(tiles, axis=1))
            pick_high = picks_high[part, g]
            both = dot(jnp.concatenate([pick_high, picks_low[part, g]], axis=0), state_high)
            read = both[0 : 2 * rows] + both[2 * rows :] + dot(pick_high, state_low)
            for j in range(group):
                at = (g * group + j) * rows
                lanes = slice(j * LANES, (j + 1) * LANES)
                sent[part, at : at + rows] = read[rows:, lanes]
                at += heads * rows
                sent[part, at : at + rows] = read[0:rows, lanes]
        sent[part, 2 * heads * rows : 2 * heads * rows + SUB] = own_lanes(sums, part, rows)
        sent_copy(part).start()

    @pl.loop(0, parts)
    def _(part):
        sent_copy(part).wait()


def owner_kernel(arrived, values, zgate, decay, beta, norm_gain, delta_out, normed_out):
    rows, heads = decay.shape
    key_heads = 2
    group = heads // key_heads
    total = arrived[0]
    for n in range(1, arrived.shape[0]):
        total = total + arrived[n]
    sums = jnp.transpose(total[2 * heads * rows :])[0:rows]
    query_scale = lax.rsqrt(1.0 + sums[:, 0:key_heads])
    key_scale = lax.rsqrt(1.0 + sums[:, key_heads : 2 * key_heads])
    unit_dot = sums[:, 2 * key_heads : 3 * key_heads] * query_scale * key_scale
    for h in range(heads):
        g = h // group
        lanes = slice(h * LANES, (h + 1) * LANES)
        d = decay[:, h : h + 1]
        ks = key_scale[:, g : g + 1]
        readk = total[h * rows : (h + 1) * rows] * ks
        delta = beta[:, h : h + 1] * (values[:, lanes] - d * readk)
        raw_q = total[(heads + h) * rows : (heads + h + 1) * rows]
        readq = d * (raw_q * query_scale[:, g : g + 1]) + unit_dot[:, g : g + 1] * delta
        meansq = jnp.mean(readq * readq, axis=1, keepdims=True)
        z = zgate[:, lanes]
        normed = readq * lax.rsqrt(meansq + 0.5) * norm_gain[...] * (z / (1.0 + jnp.exp(-z)))
        normed_out[:, lanes] = normed.astype(jnp.bfloat16)
        scaled = delta * ks
        for n in range(delta_out.shape[0]):
            delta_out[n, h * rows : (h + 1) * rows] = scaled


def update_kernel(keys, decay, delta, state_hbm, new_state, state, ready, in_sems, out_sems):
    parts, rows, heads = state.shape[0:3]
    key_heads = keys.shape[0] // SUB
    group = heads // key_heads
    span = rows * SUB

    def read(n):
        return pltpu.make_async_copy(state_hbm.at[pl.ds(n * rows, rows)], state.at[n], in_sems.at[n])

    def write(n):
        return pltpu.make_async_copy(ready.at[n], new_state.at[pl.ds(n * rows, rows)], out_sems.at[n])

    for n in range(parts):
        read(n).start()
    lane = lax.broadcasted_iota(jnp.int32, (SUB, LANES), 1)
    slot = lax.broadcasted_iota(jnp.int32, (span, LANES), 1)
    own = (slot % rows == lax.broadcasted_iota(jnp.int32, (span, LANES), 0) // SUB) & (slot < 3 * rows)
    ones = own.astype(jnp.bfloat16)
    none = jnp.zeros((LANES - 3 * rows, group * LANES), jnp.bfloat16)

    @pl.loop(0, parts)
    def _(part):
        my_keys = own_lanes(keys, part, rows)
        my_decay = decay[pl.ds(pl.multiple_of(part * rows, rows), rows)]
        read(part).wait()
        for g in range(key_heads):
            key = my_keys[g * SUB : (g + 1) * SUB]
            high = key.astype(jnp.bfloat16).astype(jnp.float32)
            low = key - high
            packed = jnp.where(lane < rows, high, jnp.where(lane < 2 * rows, pltpu.roll(low, rows, 1), pltpu.roll(high, 2 * rows, 1)))
            spread = jnp.broadcast_to(packed[None], (rows, SUB, LANES)).reshape(span, LANES)
            left = jnp.where(own, spread, 0.0).astype(jnp.bfloat16)
            own_heads = range(g * group, (g + 1) * group)
            d_high, d_low = high_low(jnp.concatenate([delta[part, h * rows : (h + 1) * rows] for h in own_heads], axis=1))
            outer = dot(left, jnp.concatenate([d_high, d_high, d_low, none], axis=0))
            wide = jnp.concatenate([jnp.broadcast_to(my_decay[:, h : h + 1], (rows, LANES)) for h in own_heads], axis=1)
            w_high = wide.astype(jnp.bfloat16)
            rest = wide - w_high.astype(jnp.float32)
            w_mid, w_low = high_low(rest)
            factor = dot(ones, jnp.concatenate([w_high, w_mid, w_low, none], axis=0))
            for j, h in enumerate(own_heads):
                lanes = slice(j * LANES, (j + 1) * LANES)
                f = factor[:, lanes].reshape(rows, SUB, LANES)
                ready[part, :, h] = f * state[part, :, h] + outer[:, lanes].reshape(rows, SUB, LANES)
        write(part).start()

    @pl.loop(0, parts)
    def _(part):
        write(part).wait()


def project_kernel(core, normed, w_out_hbm, give, keep, w_out, sem):
    copy = pltpu.make_async_copy(w_out_hbm, w_out, sem)
    copy.start()
    copy.wait()
    total = dot(normed[...], w_out[...])
    size = give.shape[2]
    first = core[0] == 0
    for y in range(give.shape[0]):
        even = total[:, 2 * y * size : (2 * y + 1) * size]
        odd = total[:, (2 * y + 1) * size : (2 * y + 2) * size]
        keep[y] = jnp.where(first, even, odd)
        give[y] = jnp.where(first, odd, even)


def chip_kernel(y, keep, got, own, *away):
    size = keep.shape[0]
    own[...] = keep[y[0]] + got[y[0]]
    for n, out in enumerate(away):
        at = (y[0] + n + 1) % size
        out[...] = keep[at] + got[at]


def head_exchange(normed, w_out, y_size):
    rows = normed.shape[0]
    heads = 2 * y_size
    size = w_out.shape[1] // heads
    head = lax.axis_index("head")
    in_smem = pl.BlockSpec(memory_space=pltpu.SMEM)
    in_vmem = pl.BlockSpec(memory_space=pltpu.VMEM)
    limit = pltpu.CompilerParams(vmem_limit_bytes=8 * 1024 * 1024)
    piece = jax.ShapeDtypeStruct((y_size, rows, size), jnp.float32)
    give, keep = pl.pallas_call(
        project_kernel,
        in_specs=[in_smem, in_vmem, pl.BlockSpec(memory_space=pl.ANY)],
        out_specs=[in_vmem, in_vmem],
        out_shape=[piece, piece],
        scratch_shapes=[pltpu.VMEM(w_out.shape, w_out.dtype), pltpu.SemaphoreType.DMA],
        compiler_params=limit,
        name="project_out",
    )((head % 2)[None], normed, pltpu.with_memory_space_constraint(w_out, pltpu.HBM))
    got = lax.ppermute(give, "head", [(h, h ^ 1) for h in range(heads)])
    total, *away = pl.pallas_call(
        chip_kernel,
        in_specs=[in_smem, in_vmem, in_vmem],
        out_specs=[in_vmem] * y_size,
        out_shape=[jax.ShapeDtypeStruct((rows, size), jnp.float32)] * y_size,
        compiler_params=limit,
        name="chip_sum",
    )((head // 2)[None], keep, got)
    for s, part in enumerate(away, 1):
        total = total + lax.ppermute(part, "head", [(h, (h + 2 * s) % heads) for h in range(heads)])
    return total


def decode(
    hidden_in,
    w_query,
    w_key,
    w_value,
    w_zgate,
    w_decay,
    w_beta,
    decay_log,
    dt_bias,
    norm_gain,
    w_out,
    state,
):
    parts = lax.axis_size("row")
    seqs, width = hidden_in.shape
    rows = seqs // parts
    heads = state.shape[1]
    key_rows = w_query.shape[1] * w_query.shape[2]
    per_part = 2 * heads * rows + SUB
    f32 = jnp.float32

    def in_hbm(value):
        return pltpu.with_memory_space_constraint(value, pltpu.HBM)

    any_space = pl.BlockSpec(memory_space=pl.ANY)
    in_vmem = pl.BlockSpec(memory_space=pltpu.VMEM)
    limit = pltpu.CompilerParams(vmem_limit_bytes=20 * 1024 * 1024)
    sent, keys, decay_all = pl.pallas_call(
        read_kernel,
        in_specs=[any_space] * 7,
        out_specs=[any_space, in_vmem, in_vmem],
        out_shape=[
            pltpu.HBM((parts, per_part, LANES), f32),
            pltpu.VMEM((key_rows, seqs), f32),
            pltpu.VMEM((seqs, heads), f32),
        ],
        scratch_shapes=[
            pltpu.VMEM((seqs, width), jnp.bfloat16),
            pltpu.VMEM((LANES, width), jnp.bfloat16),
            pltpu.VMEM((heads, width), jnp.bfloat16),
            pltpu.VMEM((1, heads), f32),
            pltpu.VMEM((1, heads), f32),
            pltpu.VMEM((parts, rows, heads, SUB, LANES), f32),
            pltpu.VMEM((parts, per_part, LANES), f32),
            pltpu.VMEM((parts, key_rows // SUB, 2 * rows, rows * SUB), jnp.bfloat16),
            pltpu.VMEM((parts, key_rows // SUB, 2 * rows, rows * SUB), jnp.bfloat16),
            pltpu.VMEM((SUB, seqs), f32),
            pltpu.SemaphoreType.DMA((6,)),
            pltpu.SemaphoreType.DMA((parts,)),
            pltpu.SemaphoreType.DMA((parts,)),
        ],
        compiler_params=limit,
        name="read_state",
    )(
        in_hbm(hidden_in),
        in_hbm(jnp.transpose(w_query, (1, 2, 0)).reshape(key_rows, width)),
        in_hbm(jnp.transpose(w_key, (1, 2, 0)).reshape(key_rows, width)),
        in_hbm(jnp.transpose(w_decay)),
        in_hbm(decay_log[None]),
        in_hbm(dt_bias[None]),
        in_hbm(state),
    )
    arrived = lax.all_to_all(sent, "row", 0, 0, tiled=True)

    own_hidden = lax.dynamic_slice_in_dim(hidden_in, lax.axis_index("row") * rows, rows, 0)
    values = jnp.einsum("bd,dhv->bhv", own_hidden, w_value, preferred_element_type=f32).reshape(rows, heads * LANES)
    zgate = jnp.einsum("bd,dhv->bhv", own_hidden, w_zgate, preferred_element_type=f32).reshape(rows, heads * LANES)
    decay_in = jnp.dot(own_hidden, w_decay, preferred_element_type=f32) + dt_bias
    decay = jnp.exp(-jnp.exp(decay_log) * jax.nn.softplus(decay_in))
    beta = jax.nn.sigmoid(jnp.dot(own_hidden, w_beta, preferred_element_type=f32))

    delta_own, normed = pl.pallas_call(
        owner_kernel,
        out_shape=[
            jax.ShapeDtypeStruct((parts, heads * rows, LANES), f32),
            jax.ShapeDtypeStruct((rows, heads * LANES), jnp.bfloat16),
        ],
        compiler_params=limit,
        name="owner_rows",
    )(arrived, values, zgate, decay, beta, norm_gain[None])
    delta = lax.all_to_all(delta_own, "row", 0, 0, tiled=True)

    layer_out = head_exchange(normed, w_out.reshape(heads * LANES, -1), lax.axis_size("head") // 2).astype(jnp.bfloat16)

    new_state = pl.pallas_call(
        update_kernel,
        in_specs=[in_vmem, in_vmem, in_vmem, any_space],
        out_specs=any_space,
        out_shape=pltpu.HBM(state.shape, f32),
        scratch_shapes=[
            pltpu.VMEM((parts, rows, heads, SUB, LANES), f32),
            pltpu.VMEM((parts, rows, heads, SUB, LANES), f32),
            pltpu.SemaphoreType.DMA((parts,)),
            pltpu.SemaphoreType.DMA((parts,)),
        ],
        compiler_params=pltpu.CompilerParams(vmem_limit_bytes=24 * 1024 * 1024),
        name="update_state",
    )(keys, decay_all, delta, in_hbm(state))
    return (layer_out, new_state)


def solution(mesh):
    in_specs = (
        P(),
        P(None, "head", "row"),
        P(None, "head", "row"),
        P(None, "head", None),
        P(None, "head", None),
        P(None, "head"),
        P(None, "head"),
        P("head"),
        P("head"),
        P(),
        P("head", None, None),
        P(None, "head", "row", None),
    )
    out_specs = (P("row", "head"), P(None, "head", "row", None))
    return jax.shard_map(decode, mesh=mesh, in_specs=in_specs, out_specs=out_specs, check_vma=False)
```

time: 107 us -> 84.3 us (0.79)
  local copies, waits for them, and re-layouts: 17.8 us -> 3.84 us
  blocking collectives: 11.8 us -> 0 us
  waiting for transfers between devices: 39 us -> 30.2 us
  Pallas kernels: 18.8 us -> 25.3 us
  starting transfers between devices: 11.7 us -> 17.6 us
    all_to_all x2, waiting for transfers between devices: 39 us -> 26 us  [the longest x1 26 us: decode(): arrived = lax.all_to_all(sent, 'row', 0, 0, tiled=True)]
    all_to_all x1 -> x0, blocking collectives: 11.8 us -> none  [local(): pieces = lax.all_to_all(pieces, 'head', 0, 0, tiled=True)]
    unnamed x32 -> x24, local copies, waits for them, and re-layouts: 12.3 us -> 3.82 us
    pallas_call x3 -> x5, Pallas kernels: 18.8 us -> 25.3 us  [the longest x1 10.6 us: decode(): pl.pallas_call(read_kernel, in_specs=[any_space] * 7, out_specs=[any_spac...]
    ppermute x0 -> x4, starting transfers between devices: none -> 5.96 us  [the longest x3 5.87 us: head_exchange(): lax.ppermute(part, 'head', [(h, (h + 2 * s) % heads) for h in range(heads)])]
    ppermute x0 -> x4, waiting for transfers between devices: none -> 4.23 us  [the longest x3 2.56 us: head_exchange(): lax.ppermute(part, 'head', [(h, (h + 2 * s) % heads) for h in range(heads)])]
    dot_general x1 -> x0, local copies, waits for them, and re-layouts: 3.92 us -> none  [local(): jnp.dot(normed, w_out.reshape(heads * LANES, -1), preferred_element_type=...]
    broadcast_in_dim x2 -> x0, local copies, waits for them, and re-layouts: 1.63 us -> none  [the longest x1 0.89 us: local(): dt_bias[:, None]]
  transfers between devices with their start and end apart: 2 -> 6, of which waited for: 2 -> 4; matrix products, arithmetic and copies ran while one was open for 9% -> 7% of each run, Pallas kernels for 0% -> 4%
where the time goes in v2:
time: 84.3 us; the launch traced here: 83.5 us
  waiting for transfers between devices  30.2 us (36%)
  Pallas kernels  25.3 us (30%)
  starting transfers between devices  17.6 us (21%)
  matrix products  5.06 us (6%)
  local copies, waits for them, and re-layouts  3.84 us (5%)
  between operations  0.87 us (1%)
    all_to_all x1, waiting for transfers between devices, decode(): arrived = lax.all_to_all(sent, 'row', 0, 0, tiled=True)  26 us
    pallas_call x1, Pallas kernels, decode(): pl.pallas_call(read_kernel, in_specs=[any_space] * 7, out_specs=[any_spac...  10.6 us
    pallas_call x1, Pallas kernels, decode(): pl.pallas_call(update_kernel, in_specs=[in_vmem, in_vmem, in_vmem, any_sp...  8.99 us
    all_to_all x1, starting transfers between devices, decode(): arrived = lax.all_to_all(sent, 'row', 0, 0, tiled=True)  8.03 us
    ppermute x3, starting transfers between devices, head_exchange(): lax.ppermute(part, 'head', [(h, (h + 2 * s) % heads) for h in range(heads)])  5.87 us
    unnamed x24, local copies, waits for them, and re-layouts  3.82 us
    all_to_all x1, starting transfers between devices, decode(): delta = lax.all_to_all(delta_own, 'row', 0, 0, tiled=True)  3.66 us
    pallas_call x1, Pallas kernels, head_exchange(): pl.pallas_call(project_kernel, in_specs=[in_smem, in_vmem, pl.BlockSpec(m...  2.71 us
  transfers between devices with their start and end apart: 6, of which 4 were waited for; matrix products, arithmetic and copies ran while one was open for 7% of the time, Pallas kernels for 4%

profile of v2, /device:TPU:0, one launch (start us, length us, event | category | flops | bytes accessed | tf_op | source)
XLA Modules:
  0.0 83.5 jit_solution(11960942374696571233)
XLA Ops:
  0.6 0.0 copy-start
  0.6 10.6 %read_state.1 = (f32[16,264,128]{2,1,0:T(8,128)}, f32[16,512]{1,0:T(8,128)S(1)}, f32[512,4]{1,0:T(8,128)S(1)}) custom-call(bf16[512,2048]{1,0:T(8,128)(2,1)} %hidden_hbm.1, bf16[16,2048]{1,0:T(8,128)(2,1)} %bitcast.30, bf16[16,2048]{1,0:T(8,128)(2,1)} %bitcast.31, bf16[4,2048]{1,0:T(4,128)(2,1)} %bitcast.32, f32[1,4]{1,0:T(1,128)} %bitcast.33, ...), custom_call_target="tpu_custom_call" | custom-call | tf_op jit(solution)/shard_map/read_state/pallas_call | solution.py:296
  11.3 0.0 copy-start.2
  11.3 0.6 copy-done.2
  11.9 8.0 %all-to-all-start = ((f32[16,264,128]{2,1,0:T(8,128)}), f32[16,264,128]{2,1,0:T(8,128)}, u32[]{:S(2)}, u32[]{:S(2)}) async-start(f32[16,264,128]{2,1,0:T(8,128)} %get-tuple-element.13), calls=%async_computation | async-start | bytes 4325376 | tf_op jit(solution)/shard_map/all_to_all | solution.py:331
  20.0 0.0 copy-done
  20.0 0.0 copy-start.10
  20.0 0.0 copy-start.8
  20.0 0.0 copy-start.11
  20.0 0.0 copy-start.7
  20.0 0.0 copy-start.9
  20.0 0.0 copy-start.6
  20.0 1.5 %fusion.4 = f32[4,4,8,128]{3,2,1,0:T(8,128)S(1)} fusion(bf16[2048,4,128]{2,1,0:T(4,128)(2,1)S(1)} %copy-done, bf16[512,2048]{1,0:T(8,128)(2,1)} %hidden_hbm.1, s32[]{:T(128)S(6)} %select_n.20), kind=kOutput, calls=%fused_computation.4 | convolution fusion | flops 67108864 | bytes 2293764 | tf_op jit(solution)/shard_map/bd,dhv->bhv/dot_general | solution.py:334
  21.5 0.1 copy-done.10
  21.6 1.4 %fusion.7 = f32[4,4,8,128]{3,2,1,0:T(8,128)S(1)} fusion(bf16[2048,4,128]{2,1,0:T(4,128)(2,1)S(1)} %copy-done.10, bf16[512,2048]{1,0:T(8,128)(2,1)} %hidden_hbm.1, s32[]{:T(128)S(6)} %select_n.20), kind=kOutput, calls=%fused_computation.5 | convolution fusion | flops 67108864 | bytes 2293764 | tf_op jit(solution)/shard_map/bd,dhv->bhv/dot_general | solution.py:335
  23.0 0.0 copy-done.8
  23.0 0.0 copy-done.11
  23.0 1.1 %fusion.12.beta = f32[32,4]{1,0:T(8,128)S(1)} fusion(bf16[2048,4]{0,1:T(4,128)(2,1)S(1)} %copy-done.11, bf16[512,2048]{1,0:T(8,128)(2,1)} %hidden_hbm.1, s32[]{:T(128)S(6)} %select_n.20), kind=kOutput, calls=%fused_computation.9 | convolution fusion | flops 524672 | bytes 147972 | tf_op jit(solution)/shard_map/dot_general | solution.py:338
  24.1 0.0 copy-done.7
  24.1 0.0 copy-done.9
  24.1 1.1 %fusion.20.decay = f32[32,4]{1,0:T(8,128)S(1)} fusion(bf16[2048,4]{0,1:T(4,128)(2,1)S(1)} %copy-done.7, bf16[512,2048]{1,0:T(8,128)(2,1)} %hidden_hbm.1, s32[]{:T(128)S(6)} %select_n.20, f32[4]{0:T(128)S(1)} %copy-done.9, f32[4]{0:T(128)S(1)} %exponential_negate_fusion), kind=kOutput, calls=%fused_computation.22 | convolution fusion | flops 525312 | bytes 148004 | tf_op jit(solution)/shard_map/dot_general | solution.py:336
  25.3 26.0 %all-to-all-done.arrived = f32[16,264,128]{2,1,0:T(8,128)} async-done(((f32[16,264,128]{2,1,0:T(8,128)}), f32[16,264,128]{2,1,0:T(8,128)}, u32[]{:S(2)}, u32[]{:S(2)}) %all-to-all-start) | async-done | bytes 2162720 | tf_op jit(solution)/shard_map/all_to_all | solution.py:331
  51.2 0.0 copy-done.6
  51.2 2.0 %owner_rows.1 = (f32[16,128,128]{2,1,0:T(8,128)S(1)}, bf16[32,512]{1,0:T(8,128)(2,1)S(1)}) custom-call(f32[16,264,128]{2,1,0:T(8,128)} %all-to-all-done.arrived, f32[32,512]{1,0:T(8,128)S(1)} %get-tuple-element.25.values, f32[32,512]{1,0:T(8,128)S(1)} %get-tuple-element.24.zgate, f32[32,4]{1,0:T(8,128)S(1)} %fusion.20.decay, f32[32,4]{1,0:T(8,128)S(1)} %fusion.12.beta, ...), custom_call_target="tpu_custom_call" | custom-call | tf_op jit(solution)/shard_map/owner_rows/pallas_call | solution.py:340
  53.3 0.0 copy-start.1
  53.3 1.0 %copy-done.1 = f32[16,128,128]{2,1,0:T(8,128)} copy-done((f32[16,128,128]{2,1,0:T(8,128)}, f32[16,128,128]{2,1,0:T(8,128)S(1)}, u32[]{:S(2)}) %copy-start.1) | copy-done | bytes 1048600
  54.3 0.0 copy-start.4
  54.3 0.6 copy-done.4
  54.9 3.7 %all-to-all-start.1 = ((f32[16,128,128]{2,1,0:T(8,128)}), f32[16,128,128]{2,1,0:T(8,128)S(1)}, u32[]{:S(2)}, u32[]{:S(2)}) async-start(f32[16,128,128]{2,1,0:T(8,128)} %copy-done.1), calls=%async_computation.1 | async-start | bytes 2097152 | tf_op jit(solution)/shard_map/all_to_all | solution.py:349
  58.6 0.0 copy-start.5
  58.6 0.7 copy-done.5
  59.3 2.7 %project_out.1 = (f32[4,32,256]{2,1,0:T(8,128)}, f32[4,32,256]{2,1,0:T(8,128)S(1)}) custom-call(s32[1]{0:T(128)} %bitcast.1.core, bf16[32,512]{1,0:T(8,128)(2,1)S(1)} %copy-done.5, bf16[512,2048]{1,0:T(8,128)(2,1)} %bitcast.29), custom_call_target="tpu_custom_call" | custom-call | tf_op jit(solution)/shard_map/project_out/pallas_call | solution.py:245
  62.0 0.1 collective-permute-start
  62.1 1.7 %collective-permute-done.got = f32[4,32,256]{2,1,0:T(8,128)} collective-permute-done((f32[4,32,256]{2,1,0:T(8,128)}, f32[4,32,256]{2,1,0:T(8,128)}, u32[]{:S(2)}, u32[]{:S(2)}) %collective-permute-start) | collective-permute-done | bytes 131104 | tf_op jit(solution)/shard_map/ppermute | solution.py:254
  63.8 0.9 %chip_sum.1 = (f32[32,256]{1,0:T(8,128)S(1)}, f32[32,256]{1,0:T(8,128)S(1)}, f32[32,256]{1,0:T(8,128)S(1)}, f32[32,256]{1,0:T(8,128)S(1)}) custom-call(s32[1]{0:T(128)} %bitcast.y, f32[4,32,256]{2,1,0:T(8,128)S(1)} %get-tuple-element.15.keep, f32[4,32,256]{2,1,0:T(8,128)} %collective-permute-done.got), custom_call_target="tpu_custom_call" | custom-call | tf_op jit(solution)/shard_map/chip_sum/pallas_call | solution.py:255
  64.7 1.6 %collective-permute-start.1 = (f32[32,256]{1,0:T(8,128)S(1)}, f32[32,256]{1,0:T(8,128)S(1)}, u32[]{:S(2)}, u32[]{:S(2)}) collective-permute-start(f32[32,256]{1,0:T(8,128)S(1)} %get-tuple-element.18), channel_id=1, source_target_pairs={{0,32},{16,48},{32,64},{48,80},{64,96},{80,112},{96,0},{112,16},{1... | collective-permute-start | bytes 98312 | tf_op jit(solution)/shard_map/ppermute | solution.py:264
  66.4 2.9 %collective-permute-start.2 = (f32[32,256]{1,0:T(8,128)S(1)}, f32[32,256]{1,0:T(8,128)S(1)}, u32[]{:S(2)}, u32[]{:S(2)}) collective-permute-start(f32[32,256]{1,0:T(8,128)S(1)} %get-tuple-element.19), channel_id=1, source_target_pairs={{0,64},{16,80},{32,96},{48,112},{64,0},{80,16},{96,32},{112,48},{1... | collective-permute-start | bytes 98312 | tf_op jit(solution)/shard_map/ppermute | solution.py:264
  69.3 1.3 %collective-permute-start.3 = (f32[32,256]{1,0:T(8,128)S(1)}, f32[32,256]{1,0:T(8,128)S(1)}, u32[]{:S(2)}, u32[]{:S(2)}) collective-permute-start(f32[32,256]{1,0:T(8,128)S(1)} %get-tuple-element.20), channel_id=1, source_target_pairs={{0,96},{16,112},{32,0},{48,16},{64,32},{80,48},{96,64},{112,80},{1... | collective-permute-start | bytes 98312 | tf_op jit(solution)/shard_map/ppermute | solution.py:264
  70.6 0.0 collective-permute-done.1
  70.6 1.2 %collective-permute-done.2 = f32[32,256]{1,0:T(8,128)S(1)} collective-permute-done((f32[32,256]{1,0:T(8,128)S(1)}, f32[32,256]{1,0:T(8,128)S(1)}, u32[]{:S(2)}, u32[]{:S(2)}) %collective-permute-start.2) | collective-permute-done | bytes 32800 | tf_op jit(solution)/shard_map/ppermute | solution.py:264
  71.8 1.4 %collective-permute-done.3 = f32[32,256]{1,0:T(8,128)S(1)} collective-permute-done((f32[32,256]{1,0:T(8,128)S(1)}, f32[32,256]{1,0:T(8,128)S(1)}, u32[]{:S(2)}, u32[]{:S(2)}) %collective-permute-start.3) | collective-permute-done | bytes 32800 | tf_op jit(solution)/shard_map/ppermute | solution.py:264
  73.2 0.6 add_convert_fusion
  73.8 0.0 all-to-all-done.1.delta
  73.8 0.0 copy-start.3
  73.8 0.8 copy-done.3
  74.5 9.0 %update_state.1 = f32[512,4,8,128]{3,2,1,0:T(8,128)} custom-call(f32[16,512]{1,0:T(8,128)S(1)} %copy-done.3, f32[512,4]{1,0:T(8,128)S(1)} %get-tuple-element.22.decay, f32[16,128,128]{2,1,0:T(8,128)S(1)} %all-to-all-done.1.delta, f32[512,4,8,128]{3,2,1,0:T(8,128)} %state_hbm.3), custom_call_target="tpu_custom_call" | custom-call | tf_op jit(solution)/shard_map/update_state/pallas_call | solution.py:353
  (2 shorter events, 0.0 us)
Async XLA Ops:
  0.6 19.3 %copy-start = (bf16[2048,4,128]{2,1,0:T(4,128)(2,1)S(1)}, bf16[2048,4,128]{2,1,0:T(4,128)(2,1)}, u32[]{:S(2)}) copy-start(bf16[2048,4,128]{2,1,0:T(4,128)(2,1)} %param.15) | copy-start | bytes 6291460
  11.3 0.6 copy-start.2
  11.9 39.3 %all-to-all-start = ((f32[16,264,128]{2,1,0:T(8,128)}), f32[16,264,128]{2,1,0:T(8,128)}, u32[]{:S(2)}, u32[]{:S(2)}) async-start(f32[16,264,128]{2,1,0:T(8,128)} %get-tuple-element.13), calls=%async_computation | async-start | bytes 4325376 | tf_op jit(solution)/shard_map/all_to_all | solution.py:331
  20.0 1.7 %copy-start.10 = (bf16[2048,4,128]{2,1,0:T(4,128)(2,1)S(1)}, bf16[2048,4,128]{2,1,0:T(4,128)(2,1)}, u32[]{:S(2)}) copy-start(bf16[2048,4,128]{2,1,0:T(4,128)(2,1)} %param.16) | copy-start | bytes 6291460
  20.0 3.0 %copy-start.8 = (f32[4]{0:T(128)S(1)}, f32[4]{0:T(128)}, u32[]{:S(2)}) copy-start(f32[4]{0:T(128)} %param.19) | copy-start | bytes 52
  20.0 3.0 %copy-start.11 = (bf16[2048,4]{0,1:T(4,128)(2,1)S(1)}, bf16[2048,4]{0,1:T(4,128)(2,1)}, u32[]{:S(2)}) copy-start(bf16[2048,4]{0,1:T(4,128)(2,1)} %param.18) | copy-start | bytes 49156
  20.0 4.1 %copy-start.7 = (bf16[2048,4]{0,1:T(4,128)(2,1)S(1)}, bf16[2048,4]{0,1:T(4,128)(2,1)}, u32[]{:S(2)}) copy-start(bf16[2048,4]{0,1:T(4,128)(2,1)} %param.17) | copy-start | bytes 49156
  20.0 4.1 %copy-start.9 = (f32[4]{0:T(128)S(1)}, f32[4]{0:T(128)}, u32[]{:S(2)}) copy-start(f32[4]{0:T(128)} %param.20) | copy-start | bytes 52
  20.0 31.2 %copy-start.6 = (f32[128]{0:T(128)S(1)}, f32[128]{0:T(128)}, u32[]{:S(2)}) copy-start(f32[128]{0:T(128)} %param.21) | copy-start | bytes 1540
  53.3 1.0 %copy-start.1 = (f32[16,128,128]{2,1,0:T(8,128)}, f32[16,128,128]{2,1,0:T(8,128)S(1)}, u32[]{:S(2)}) copy-start(f32[16,128,128]{2,1,0:T(8,128)S(1)} %get-tuple-element.23) | copy-start | bytes 3145732
  54.3 0.6 copy-start.4
  54.9 18.9 %all-to-all-start.1 = ((f32[16,128,128]{2,1,0:T(8,128)}), f32[16,128,128]{2,1,0:T(8,128)S(1)}, u32[]{:S(2)}, u32[]{:S(2)}) async-start(f32[16,128,128]{2,1,0:T(8,128)} %copy-done.1), calls=%async_computation.1 | async-start | bytes 2097152 | tf_op jit(solution)/shard_map/all_to_all | solution.py:349
  58.6 0.8 copy-start.5
  62.0 1.8 %collective-permute-start = (f32[4,32,256]{2,1,0:T(8,128)}, f32[4,32,256]{2,1,0:T(8,128)}, u32[]{:S(2)}, u32[]{:S(2)}) collective-permute-start(f32[4,32,256]{2,1,0:T(8,128)} %get-tuple-element.16), channel_id=1, source_target_pairs={{0,16},{16,0},{32,48},{48,32},{64,80},{80,64},{96,112},{112,96},{1... | collective-permute-start | bytes 393224 | tf_op jit(solution)/shard_map/ppermute | solution.py:254
  64.7 5.9 %collective-permute-start.1 = (f32[32,256]{1,0:T(8,128)S(1)}, f32[32,256]{1,0:T(8,128)S(1)}, u32[]{:S(2)}, u32[]{:S(2)}) collective-permute-start(f32[32,256]{1,0:T(8,128)S(1)} %get-tuple-element.18), channel_id=1, source_target_pairs={{0,32},{16,48},{32,64},{48,80},{64,96},{80,112},{96,0},{112,16},{1... | collective-permute-start | bytes 98312 | tf_op jit(solution)/shard_map/ppermute | solution.py:264
  66.4 5.4 %collective-permute-start.2 = (f32[32,256]{1,0:T(8,128)S(1)}, f32[32,256]{1,0:T(8,128)S(1)}, u32[]{:S(2)}, u32[]{:S(2)}) collective-permute-start(f32[32,256]{1,0:T(8,128)S(1)} %get-tuple-element.19), channel_id=1, source_target_pairs={{0,64},{16,80},{32,96},{48,112},{64,0},{80,16},{96,32},{112,48},{1... | collective-permute-start | bytes 98312 | tf_op jit(solution)/shard_map/ppermute | solution.py:264
  69.3 3.9 %collective-permute-start.3 = (f32[32,256]{1,0:T(8,128)S(1)}, f32[32,256]{1,0:T(8,128)S(1)}, u32[]{:S(2)}, u32[]{:S(2)}) collective-permute-start(f32[32,256]{1,0:T(8,128)S(1)} %get-tuple-element.20), channel_id=1, source_target_pairs={{0,96},{16,112},{32,0},{48,16},{64,32},{80,48},{96,64},{112,80},{1... | collective-permute-start | bytes 98312 | tf_op jit(solution)/shard_map/ppermute | solution.py:264
  73.8 0.8 copy-start.3

commit v3 on v2

v3 whole, which is shorter than its diff:
```python
import jax
import jax.numpy as jnp
from jax import lax
from jax.experimental import pallas as pl
from jax.experimental.pallas import tpu as pltpu
from jax.sharding import PartitionSpec as P


LANES = 128
SUB = 8


def high_low(value):
    high = value.astype(jnp.bfloat16)
    return high, (value - high.astype(jnp.float32)).astype(jnp.bfloat16)


def dot(left, right):
    return jnp.dot(left, right, preferred_element_type=jnp.float32)


def read_kernel(
    hidden_hbm,
    w_query_hbm,
    w_key_hbm,
    w_decay_hbm,
    decay_log_hbm,
    dt_bias_hbm,
    state_hbm,
    sent_hbm,
    keys_hbm,
    decay_hbm,
    hidden,
    weights,
    w_decay,
    decay_log,
    dt_bias,
    state,
    sent,
    picks,
    sums,
    keys_all,
    decay_all,
    in_sems,
    hidden_sems,
    state_sems,
    sent_sems,
    out_sems,
):
    parts, rows, heads = state.shape[0:3]
    chunks = hidden.shape[0]
    per_chunk = parts // chunks
    key_rows = w_query_hbm.shape[0]
    key_heads = key_rows // SUB
    group = heads // key_heads
    span = rows * SUB
    pad = weights.dtype.itemsize * SUB

    inputs = [
        pltpu.make_async_copy(w_query_hbm, weights.at[pad : pad + key_rows], in_sems.at[0]),
        pltpu.make_async_copy(w_key_hbm, weights.at[pad + key_rows : pad + 2 * key_rows], in_sems.at[1]),
        pltpu.make_async_copy(w_decay_hbm, w_decay, in_sems.at[2]),
        pltpu.make_async_copy(decay_log_hbm, decay_log, in_sems.at[3]),
        pltpu.make_async_copy(dt_bias_hbm, dt_bias, in_sems.at[4]),
    ]
    for copy in inputs:
        copy.start()

    def hidden_copy(n):
        return pltpu.make_async_copy(hidden_hbm.at[pl.ds(n * LANES, LANES)], hidden.at[n], hidden_sems.at[n])

    def state_copy(n):
        return pltpu.make_async_copy(state_hbm.at[pl.ds(n * rows, rows)], state.at[n], state_sems.at[n])

    def sent_copy(n):
        return pltpu.make_async_copy(sent.at[n], sent_hbm.at[n], sent_sems.at[n])

    ahead = 8
    for n in range(chunks):
        hidden_copy(n).start()
    width = weights.shape[1]
    weights[0:pad] = jnp.zeros((pad, width), weights.dtype)
    weights[pad + 2 * key_rows :] = jnp.zeros((LANES - pad - 2 * key_rows, width), weights.dtype)
    sums[...] = jnp.zeros(sums.shape, sums.dtype)
    source = lax.broadcasted_iota(jnp.int32, (LANES, span), 0)
    entry = lax.broadcasted_iota(jnp.int32, (LANES, span), 1) % SUB
    own = lax.broadcasted_iota(jnp.int32, (rows, span), 1) // SUB == lax.broadcasted_iota(jnp.int32, (rows, span), 0)
    for n in range(2 * key_heads):
        picks[n] = (source == pad + n * SUB + entry).astype(jnp.bfloat16)
    for copy in inputs:
        copy.wait()
    weights[0:heads] = w_decay[...]

    @pl.loop(0, chunks)
    def _(chunk):
        hidden_copy(chunk).wait()

        @pl.when(chunk == 0)
        def _():
            for n in range(ahead):
                state_copy(n).start()

        projected = lax.dot_general(hidden[chunk], weights[...], (((1,), (1,)), ((), ())), preferred_element_type=jnp.float32)
        halves = jnp.concatenate(high_low(projected), axis=0)
        left = []
        for n in range(2 * key_heads):
            wide = dot(halves, picks[n]).reshape(2 * per_chunk, rows, span)
            left.append(jnp.where(own[None], wide, 0.0).astype(jnp.bfloat16))

        at = pl.multiple_of(chunk * LANES, LANES)
        pre = projected[:, 0:heads] + dt_bias[...]
        soft = jnp.maximum(pre, 0.0) + jnp.log1p(jnp.exp(-jnp.abs(pre)))
        decay_all[pl.ds(at, LANES)] = jnp.exp(-jnp.exp(decay_log[...]) * soft)
        turned = jnp.transpose(projected)
        query = turned[pad : pad + key_rows]
        keys = turned[pad + key_rows : pad + 2 * key_rows]
        keys_all[:, pl.ds(at, LANES)] = keys
        for n, product in enumerate((query * query, keys * keys, query * keys)):
            for g in range(key_heads):
                sums[n * key_heads + g : n * key_heads + g + 1] = jnp.sum(product[g * SUB : (g + 1) * SUB], axis=0, keepdims=True)

        for p in range(per_chunk):
            part = chunk * per_chunk + p
            state_copy(part).wait()

            @pl.when(part + ahead < parts)
            def _():
                state_copy(part + ahead).start()

            for g in range(key_heads):
                tiles = [state[part, :, g * group + j].reshape(span, LANES) for j in range(group)]
                state_high, state_low = high_low(jnp.concatenate(tiles, axis=1))
                q_left, k_left = left[g], left[key_heads + g]
                high = jnp.concatenate([q_left[p], k_left[p]], axis=0)
                both = dot(jnp.concatenate([high, q_left[per_chunk + p], k_left[per_chunk + p]], axis=0), state_high)
                read = both[0 : 2 * rows] + both[2 * rows :] + dot(high, state_low)
                for j in range(group):
                    to = (g * group + j) * rows
                    lanes = slice(j * LANES, (j + 1) * LANES)
                    sent[part, to : to + rows] = read[rows:, lanes]
                    to += heads * rows
                    sent[part, to : to + rows] = read[0:rows, lanes]
            to = 2 * heads * rows
            sent[part, to : to + SUB] = pltpu.roll(sums[...], (LANES - p * rows) % LANES, 1)
            sent_copy(part).start()

    outputs = [
        pltpu.make_async_copy(keys_all, keys_hbm, out_sems.at[0]),
        pltpu.make_async_copy(decay_all, decay_hbm, out_sems.at[1]),
    ]
    for copy in outputs:
        copy.start()

    @pl.loop(0, parts)
    def _(part):
        sent_copy(part).wait()

    for copy in outputs:
        copy.wait()


def owner_kernel(arrived, values, zgate, decay, beta, norm_gain, delta_out, normed_out):
    rows, heads = decay.shape
    key_heads = 2
    group = heads // key_heads
    total = arrived[0]
    for n in range(1, arrived.shape[0]):
        total = total + arrived[n]
    sums = jnp.transpose(total[2 * heads * rows :])[0:rows]
    query_scale = lax.rsqrt(1.0 + sums[:, 0:key_heads])
    key_scale = lax.rsqrt(1.0 + sums[:, key_heads : 2 * key_heads])
    unit_dot = sums[:, 2 * key_heads : 3 * key_heads] * query_scale * key_scale
    for h in range(heads):
        g = h // group
        lanes = slice(h * LANES, (h + 1) * LANES)
        d = decay[:, h : h + 1]
        ks = key_scale[:, g : g + 1]
        readk = total[h * rows : (h + 1) * rows] * ks
        delta = beta[:, h : h + 1] * (values[:, lanes] - d * readk)
        raw_q = total[(heads + h) * rows : (heads + h + 1) * rows]
        readq = d * (raw_q * query_scale[:, g : g + 1]) + unit_dot[:, g : g + 1] * delta
        meansq = jnp.mean(readq * readq, axis=1, keepdims=True)
        z = zgate[:, lanes]
        normed = readq * lax.rsqrt(meansq + 0.5) * norm_gain[...] * (z / (1.0 + jnp.exp(-z)))
        normed_out[:, lanes] = normed.astype(jnp.bfloat16)
        scaled = delta * ks
        for n in range(delta_out.shape[0]):
            delta_out[n, h * rows : (h + 1) * rows] = scaled


def update_kernel(delta, keys_hbm, decay_hbm, state_hbm, new_state, keys, decay, wide, state, ready, small_sems, in_sems, out_sems):
    parts, rows, heads = state.shape[0:3]
    key_heads = keys.shape[0] // SUB
    group = heads // key_heads
    span = rows * SUB
    per_tile = LANES // rows
    together = 4

    small = [
        pltpu.make_async_copy(decay_hbm, decay, small_sems.at[0]),
        pltpu.make_async_copy(keys_hbm, keys, small_sems.at[1]),
    ]
    for copy in small:
        copy.start()

    def read(n):
        return pltpu.make_async_copy(state_hbm.at[pl.ds(n * rows, rows)], state.at[n], in_sems.at[n])

    def write(n):
        return pltpu.make_async_copy(ready.at[n], new_state.at[pl.ds(n * rows, rows)], out_sems.at[n])

    ahead = 6
    for n in range(ahead):
        read(n).start()
    lane = lax.broadcasted_iota(jnp.int32, (SUB, LANES), 1)
    slot = lax.broadcasted_iota(jnp.int32, (span, LANES), 1)
    own = (slot % rows == lax.broadcasted_iota(jnp.int32, (span, LANES), 0) // SUB) & (slot < 3 * rows)
    ones = jnp.ones((LANES, LANES), jnp.bfloat16)
    for copy in small:
        copy.wait()

    @pl.loop(0, parts // per_tile)
    def _(n):
        at = pl.multiple_of(n * LANES, LANES)
        some = decay[pl.ds(at, LANES)]
        for h in range(heads):
            spread = jnp.broadcast_to(some[:, h : h + 1], (LANES, LANES)).reshape(per_tile, rows, LANES)
            wide[pl.ds(n * per_tile, per_tile), :, h * LANES : (h + 1) * LANES] = spread

    @pl.loop(0, parts // together)
    def _(pair):
        tile = keys[:, pl.ds(pl.multiple_of(pair * together // per_tile * LANES, LANES), LANES)]
        for n in range(together):
            part = pair * together + n
            key = pltpu.roll(tile, (LANES - part % per_tile * rows) % LANES, 1)
            high = key.astype(jnp.bfloat16).astype(jnp.float32)
            rest = key - high
            middle = rest.astype(jnp.bfloat16).astype(jnp.float32)
            low = pltpu.roll(rest - middle, 2 * rows, 1)
            packed = jnp.where(lane[0:1] < rows, high, jnp.where(lane[0:1] < 2 * rows, pltpu.roll(middle, rows, 1), low))
            read(part).wait()

            @pl.when(part + ahead < parts)
            def _():
                read(part + ahead).start()

            for g in range(key_heads):
                spread = jnp.broadcast_to(packed[None, g * SUB : (g + 1) * SUB], (rows, SUB, LANES)).reshape(span, LANES)
                wide_key = dot(jnp.where(own, spread, 0.0).astype(jnp.bfloat16), ones)
                for b in range(rows):
                    k = wide_key[b * SUB : (b + 1) * SUB]
                    for h in range(g * group, (g + 1) * group):
                        row = jnp.broadcast_to(delta[part, h * rows + b : h * rows + b + 1], (SUB, LANES))
                        factor = jnp.broadcast_to(wide[part, b : b + 1, h * LANES : (h + 1) * LANES], (SUB, LANES))
                        ready[part, b, h] = factor * state[part, b, h] + k * row
            write(part).start()

    @pl.loop(0, parts)
    def _(part):
        write(part).wait()


def project_kernel(core, normed, w_out_hbm, give, keep, w_out, sem):
    copy = pltpu.make_async_copy(w_out_hbm, w_out, sem)
    copy.start()
    copy.wait()
    total = dot(normed[...], w_out[...])
    size = give.shape[2]
    first = core[0] == 0
    for y in range(give.shape[0]):
        even = total[:, 2 * y * size : (2 * y + 1) * size]
        odd = total[:, (2 * y + 1) * size : (2 * y + 2) * size]
        keep[y] = jnp.where(first, even, odd)
        give[y] = jnp.where(first, odd, even)


def chip_kernel(y, keep, got, own, *away):
    size = keep.shape[0]
    own[...] = keep[y[0]] + got[y[0]]
    for n, out in enumerate(away):
        at = (y[0] + n + 1) % size
        out[...] = keep[at] + got[at]


def head_exchange(normed, w_out, y_size):
    rows = normed.shape[0]
    heads = 2 * y_size
    size = w_out.shape[1] // heads
    head = lax.axis_index("head")
    in_smem = pl.BlockSpec(memory_space=pltpu.SMEM)
    in_vmem = pl.BlockSpec(memory_space=pltpu.VMEM)
    limit = pltpu.CompilerParams(vmem_limit_bytes=8 * 1024 * 1024)
    piece = jax.ShapeDtypeStruct((y_size, rows, size), jnp.float32)
    give, keep = pl.pallas_call(
        project_kernel,
        in_specs=[in_smem, in_vmem, pl.BlockSpec(memory_space=pl.ANY)],
        out_specs=[in_vmem, in_vmem],
        out_shape=[piece, piece],
        scratch_shapes=[pltpu.VMEM(w_out.shape, w_out.dtype), pltpu.SemaphoreType.DMA],
        compiler_params=limit,
        name="project_out",
    )((head % 2)[None], normed, pltpu.with_memory_space_constraint(w_out, pltpu.HBM))
    got = lax.ppermute(give, "head", [(h, h ^ 1) for h in range(heads)])
    total, *away = pl.pallas_call(
        chip_kernel,
        in_specs=[in_smem, in_vmem, in_vmem],
        out_specs=[in_vmem] * y_size,
        out_shape=[jax.ShapeDtypeStruct((rows, size), jnp.float32)] * y_size,
        compiler_params=limit,
        name="chip_sum",
    )((head // 2)[None], keep, got)
    for s, part in enumerate(away, 1):
        total = total + lax.ppermute(part, "head", [(h, (h + 2 * s) % heads) for h in range(heads)])
    return total


def decode(
    hidden_in,
    w_query,
    w_key,
    w_value,
    w_zgate,
    w_decay,
    w_beta,
    decay_log,
    dt_bias,
    norm_gain,
    w_out,
    state,
):
    parts = lax.axis_size("row")
    seqs, width = hidden_in.shape
    rows = seqs // parts
    heads = state.shape[1]
    key_rows = w_query.shape[1] * w_query.shape[2]
    per_part = 2 * heads * rows + SUB
    f32 = jnp.float32

    def in_hbm(value):
        return pltpu.with_memory_space_constraint(value, pltpu.HBM)

    any_space = pl.BlockSpec(memory_space=pl.ANY)
    in_vmem = pl.BlockSpec(memory_space=pltpu.VMEM)
    limit = pltpu.CompilerParams(vmem_limit_bytes=20 * 1024 * 1024)
    sent, keys, decay_all = pl.pallas_call(
        read_kernel,
        in_specs=[any_space] * 7,
        out_specs=[any_space] * 3,
        out_shape=[
            pltpu.HBM((parts, per_part, LANES), f32),
            pltpu.HBM((key_rows, seqs), f32),
            pltpu.HBM((seqs, heads), f32),
        ],
        scratch_shapes=[
            pltpu.VMEM((seqs // LANES, LANES, width), jnp.bfloat16),
            pltpu.VMEM((LANES, width), jnp.bfloat16),
            pltpu.VMEM((heads, width), jnp.bfloat16),
            pltpu.VMEM((1, heads), f32),
            pltpu.VMEM((1, heads), f32),
            pltpu.VMEM((parts, rows, heads, SUB, LANES), f32),
            pltpu.VMEM((parts, per_part, LANES), f32),
            pltpu.VMEM((2 * key_rows // SUB, LANES, rows * SUB), jnp.bfloat16),
            pltpu.VMEM((SUB, LANES), f32),
            pltpu.VMEM((key_rows, seqs), f32),
            pltpu.VMEM((seqs, heads), f32),
            pltpu.SemaphoreType.DMA((5,)),
            pltpu.SemaphoreType.DMA((seqs // LANES,)),
            pltpu.SemaphoreType.DMA((parts,)),
            pltpu.SemaphoreType.DMA((parts,)),
            pltpu.SemaphoreType.DMA((2,)),
        ],
        compiler_params=limit,
        name="read_state",
    )(
        in_hbm(hidden_in),
        in_hbm(jnp.transpose(w_query, (1, 2, 0)).reshape(key_rows, width)),
        in_hbm(jnp.transpose(w_key, (1, 2, 0)).reshape(key_rows, width)),
        in_hbm(jnp.transpose(w_decay)),
        in_hbm(decay_log[None]),
        in_hbm(dt_bias[None]),
        in_hbm(state),
    )
    arrived = lax.all_to_all(sent, "row", 0, 0, tiled=True)

    own_hidden = lax.dynamic_slice_in_dim(hidden_in, lax.axis_index("row") * rows, rows, 0)
    values = jnp.einsum("bd,dhv->bhv", own_hidden, w_value, preferred_element_type=f32).reshape(rows, heads * LANES)
    zgate = jnp.einsum("bd,dhv->bhv", own_hidden, w_zgate, preferred_element_type=f32).reshape(rows, heads * LANES)
    decay_in = jnp.dot(own_hidden, w_decay, preferred_element_type=f32) + dt_bias
    decay = jnp.exp(-jnp.exp(decay_log) * jax.nn.softplus(decay_in))
    beta = jax.nn.sigmoid(jnp.dot(own_hidden, w_beta, preferred_element_type=f32))

    delta_own, normed = pl.pallas_call(
        owner_kernel,
        out_shape=[
            pltpu.VMEM((parts, heads * rows, LANES), f32),
            pltpu.VMEM((rows, heads * LANES), jnp.bfloat16),
        ],
        compiler_params=limit,
        name="owner_rows",
    )(arrived, values, zgate, decay, beta, norm_gain[None])
    delta = lax.all_to_all(delta_own, "row", 0, 0, tiled=True)

    layer_out = head_exchange(normed, w_out.reshape(heads * LANES, -1), lax.axis_size("head") // 2).astype(jnp.bfloat16)

    new_state = pl.pallas_call(
        update_kernel,
        in_specs=[in_vmem, any_space, any_space, any_space],
        out_specs=any_space,
        out_shape=pltpu.HBM(state.shape, f32),
        scratch_shapes=[
            pltpu.VMEM((key_rows, seqs), f32),
            pltpu.VMEM((seqs, heads), f32),
            pltpu.VMEM((parts, rows, heads * LANES), f32),
            pltpu.VMEM((parts, rows, heads, SUB, LANES), f32),
            pltpu.VMEM((parts, rows, heads, SUB, LANES), f32),
            pltpu.SemaphoreType.DMA((2,)),
            pltpu.SemaphoreType.DMA((parts,)),
            pltpu.SemaphoreType.DMA((parts,)),
        ],
        compiler_params=pltpu.CompilerParams(vmem_limit_bytes=24 * 1024 * 1024),
        name="update_state",
    )(delta, in_hbm(keys), in_hbm(decay_all), in_hbm(state))
    return (layer_out, new_state)


def solution(mesh):
    in_specs = (
        P(),
        P(None, "head", "row"),
        P(None, "head", "row"),
        P(None, "head", None),
        P(None, "head", None),
        P(None, "head"),
        P(None, "head"),
        P("head"),
        P("head"),
        P(),
        P("head", None, None),
        P(None, "head", "row", None),
    )
    out_specs = (P("row", "head"), P(None, "head", "row", None))
    return jax.shard_map(decode, mesh=mesh, in_specs=in_specs, out_specs=out_specs, check_vma=False)
```

time: 84.3 us -> 79.8 us (0.947)
  Pallas kernels: 25.3 us -> 21.8 us
  local copies, waits for them, and re-layouts: 3.84 us -> 1.1 us
  waiting for transfers between devices: 30.2 us -> 32.3 us
    unnamed x24 -> x16, local copies, waits for them, and re-layouts: 3.82 us -> 1.09 us
    all_to_all x1, waiting for transfers between devices: 0.01 us -> 2.39 us  [decode(): delta = lax.all_to_all(delta_own, 'row', 0, 0, tiled=True)]
    pallas_call x1, Pallas kernels: 10.6 us -> 9.56 us  [decode(): pl.pallas_call(read_kernel, in_specs=[any_space] * 7, out_specs=[any_spac...]
    pallas_call x1, Pallas kernels: 0.92 us -> 0.02 us  [head_exchange(): pl.pallas_call(chip_kernel, in_specs=[in_smem, in_vmem, in_vmem], out_spe...]
    pallas_call x2, Pallas kernels: 11 us -> 10.1 us  [the longest x1 8.11 us: decode(): pl.pallas_call(update_kernel, in_specs=[in_vmem, any_space, any_space, an...]
  transfers between devices with their start and end apart: 6 -> 6, of which waited for: 4 -> 5; matrix products, arithmetic and copies ran while one was open for 7% -> 7% of each run, Pallas kernels for 4% -> 3%
where the time goes in v3:
time: 79.8 us; the launch traced here: 79.4 us
  waiting for transfers between devices  32.3 us (40%)
  Pallas kernels  21.8 us (27%)
  starting transfers between devices  17.7 us (22%)
  matrix products  5.05 us (6%)
  local copies, waits for them, and re-layouts  1.1 us (1%)
  between operations  0.85 us (1%)
    all_to_all x1, waiting for transfers between devices, decode(): arrived = lax.all_to_all(sent, 'row', 0, 0, tiled=True)  26 us
    pallas_call x1, Pallas kernels, decode(): pl.pallas_call(read_kernel, in_specs=[any_space] * 7, out_specs=[any_spac...  9.56 us
    pallas_call x1, Pallas kernels, decode(): pl.pallas_call(update_kernel, in_specs=[in_vmem, any_space, any_space, an...  8.11 us
    all_to_all x1, starting transfers between devices, decode(): arrived = lax.all_to_all(sent, 'row', 0, 0, tiled=True)  8.05 us
    ppermute x3, starting transfers between devices, head_exchange(): lax.ppermute(part, 'head', [(h, (h + 2 * s) % heads) for h in range(heads)])  5.9 us
    all_to_all x1, starting transfers between devices, decode(): delta = lax.all_to_all(delta_own, 'row', 0, 0, tiled=True)  3.66 us
    ppermute x3, waiting for transfers between devices, head_exchange(): lax.ppermute(part, 'head', [(h, (h + 2 * s) % heads) for h in range(heads)])  2.56 us
    all_to_all x1, waiting for transfers between devices, decode(): delta = lax.all_to_all(delta_own, 'row', 0, 0, tiled=True)  2.39 us
  transfers between devices with their start and end apart: 6, of which 5 were waited for; matrix products, arithmetic and copies ran while one was open for 7% of the time, Pallas kernels for 3%

profile of v3, /device:TPU:0, one launch (start us, length us, event | category | flops | bytes accessed | tf_op | source)
XLA Modules:
  0.0 79.4 jit_solution(1140952224878402277)
XLA Ops:
  0.6 0.0 copy-start
  0.6 9.6 %read_state.1 = (f32[16,264,128]{2,1,0:T(8,128)}, f32[16,512]{1,0:T(8,128)}, f32[512,4]{1,0:T(8,128)}) custom-call(bf16[512,2048]{1,0:T(8,128)(2,1)} %hidden_hbm.1, bf16[16,2048]{1,0:T(8,128)(2,1)} %bitcast.30, bf16[16,2048]{1,0:T(8,128)(2,1)} %bitcast.31, bf16[4,2048]{1,0:T(4,128)(2,1)} %bitcast.32, f32[1,4]{1,0:T(1,128)} %bitcast.33, f32[1,4]{1,0:T(1,128)} %bitcast.34, ...), custom_call_target="tpu_custom_call" | custom-call | tf_op jit(solution)/shard_map/read_state/pallas_call | solution.py:345
  10.2 8.0 %all-to-all-start = ((f32[16,264,128]{2,1,0:T(8,128)}), f32[16,264,128]{2,1,0:T(8,128)}, u32[]{:S(2)}, u32[]{:S(2)}) async-start(f32[16,264,128]{2,1,0:T(8,128)} %get-tuple-element.13), calls=%async_computation | async-start | bytes 4325376 | tf_op jit(solution)/shard_map/all_to_all | solution.py:383
  18.3 0.0 copy-done
  18.3 0.0 copy-start.6
  18.3 0.0 copy-start.4
  18.3 0.0 copy-start.7
  18.3 0.0 copy-start.3
  18.3 0.0 copy-start.5
  18.3 0.0 copy-start.2
  18.4 1.5 %fusion.4 = f32[4,4,8,128]{3,2,1,0:T(8,128)S(1)} fusion(bf16[2048,4,128]{2,1,0:T(4,128)(2,1)S(1)} %copy-done, bf16[512,2048]{1,0:T(8,128)(2,1)} %hidden_hbm.1, s32[]{:T(128)S(6)} %select_n.20), kind=kOutput, calls=%fused_computation.4 | convolution fusion | flops 67108864 | bytes 2293764 | tf_op jit(solution)/shard_map/bd,dhv->bhv/dot_general | solution.py:386
  19.9 0.1 copy-done.6
  19.9 1.4 %fusion.7 = f32[4,4,8,128]{3,2,1,0:T(8,128)S(1)} fusion(bf16[2048,4,128]{2,1,0:T(4,128)(2,1)S(1)} %copy-done.6, bf16[512,2048]{1,0:T(8,128)(2,1)} %hidden_hbm.1, s32[]{:T(128)S(6)} %select_n.20), kind=kOutput, calls=%fused_computation.5 | convolution fusion | flops 67108864 | bytes 2293764 | tf_op jit(solution)/shard_map/bd,dhv->bhv/dot_general | solution.py:387
  21.3 0.0 copy-done.4
  21.3 0.0 copy-done.7
  21.3 1.1 %fusion.12.beta = f32[32,4]{1,0:T(8,128)S(1)} fusion(bf16[2048,4]{0,1:T(4,128)(2,1)S(1)} %copy-done.7, bf16[512,2048]{1,0:T(8,128)(2,1)} %hidden_hbm.1, s32[]{:T(128)S(6)} %select_n.20), kind=kOutput, calls=%fused_computation.9 | convolution fusion | flops 524672 | bytes 147972 | tf_op jit(solution)/shard_map/dot_general | solution.py:390
  22.4 0.0 copy-done.3
  22.4 0.0 copy-done.5
  22.5 1.1 %fusion.20.decay = f32[32,4]{1,0:T(8,128)S(1)} fusion(bf16[2048,4]{0,1:T(4,128)(2,1)S(1)} %copy-done.3, bf16[512,2048]{1,0:T(8,128)(2,1)} %hidden_hbm.1, s32[]{:T(128)S(6)} %select_n.20, f32[4]{0:T(128)S(1)} %copy-done.5, f32[4]{0:T(128)S(1)} %exponential_negate_fusion), kind=kOutput, calls=%fused_computation.22 | convolution fusion | flops 525312 | bytes 148004 | tf_op jit(solution)/shard_map/dot_general | solution.py:388
  23.6 26.0 %all-to-all-done.arrived = f32[16,264,128]{2,1,0:T(8,128)} async-done(((f32[16,264,128]{2,1,0:T(8,128)}), f32[16,264,128]{2,1,0:T(8,128)}, u32[]{:S(2)}, u32[]{:S(2)}) %all-to-all-start) | async-done | bytes 2162720 | tf_op jit(solution)/shard_map/all_to_all | solution.py:383
  49.6 0.0 copy-done.2
  49.6 2.0 %owner_rows.1 = (f32[16,128,128]{2,1,0:T(8,128)S(1)}, bf16[32,512]{1,0:T(8,128)(2,1)S(1)}) custom-call(f32[16,264,128]{2,1,0:T(8,128)} %all-to-all-done.arrived, f32[32,512]{1,0:T(8,128)S(1)} %get-tuple-element.25.values, f32[32,512]{1,0:T(8,128)S(1)} %get-tuple-element.24.zgate, f32[32,4]{1,0:T(8,128)S(1)} %fusion.20.decay, f32[32,4]{1,0:T(8,128)S(1)} %fusion.12.beta, ...), custom_call_target="tpu_custom_call" | custom-call | tf_op jit(solution)/shard_map/owner_rows/pallas_call | solution.py:392
  51.6 0.0 copy-start.1
  51.6 1.0 %copy-done.1 = f32[16,128,128]{2,1,0:T(8,128)} copy-done((f32[16,128,128]{2,1,0:T(8,128)}, f32[16,128,128]{2,1,0:T(8,128)S(1)}, u32[]{:S(2)}) %copy-start.1) | copy-done | bytes 1048600
  52.6 3.7 %all-to-all-start.1 = ((f32[16,128,128]{2,1,0:T(8,128)}), f32[16,128,128]{2,1,0:T(8,128)S(1)}, u32[]{:S(2)}, u32[]{:S(2)}) async-start(f32[16,128,128]{2,1,0:T(8,128)} %copy-done.1), calls=%async_computation.1 | async-start | bytes 2097152 | tf_op jit(solution)/shard_map/all_to_all | solution.py:401
  56.2 2.1 %project_out.1 = (f32[4,32,256]{2,1,0:T(8,128)S(1)}, f32[4,32,256]{2,1,0:T(8,128)S(1)}) custom-call(s32[1]{0:T(128)} %bitcast.1.core, bf16[32,512]{1,0:T(8,128)(2,1)S(1)} %get-tuple-element.14.normed, bf16[512,2048]{1,0:T(8,128)(2,1)} %bitcast.29), custom_call_target="tpu_custom_call" | custom-call | tf_op jit(solution)/shard_map/project_out/pallas_call | solution.py:294
  58.3 0.1 collective-permute-start
  58.4 1.3 %collective-permute-done.got = f32[4,32,256]{2,1,0:T(8,128)S(1)} collective-permute-done((f32[4,32,256]{2,1,0:T(8,128)S(1)}, f32[4,32,256]{2,1,0:T(8,128)S(1)}, u32[]{:S(2)}, u32[]{:S(2)}) %collective-permute-start) | collective-permute-done | bytes 131104 | tf_op jit(solution)/shard_map/ppermute | solution.py:303
  59.8 1.6 %collective-permute-start.1 = (f32[32,256]{1,0:T(8,128)S(1)}, f32[32,256]{1,0:T(8,128)S(1)}, u32[]{:S(2)}, u32[]{:S(2)}) collective-permute-start(f32[32,256]{1,0:T(8,128)S(1)} %get-tuple-element.18), channel_id=1, source_target_pairs={{0,32},{16,48},{32,64},{48,80},{64,96},{80,112},{96,0},{112,16},{1... | collective-permute-start | bytes 98312 | tf_op jit(solution)/shard_map/ppermute | solution.py:313
  61.4 2.9 %collective-permute-start.2 = (f32[32,256]{1,0:T(8,128)S(1)}, f32[32,256]{1,0:T(8,128)S(1)}, u32[]{:S(2)}, u32[]{:S(2)}) collective-permute-start(f32[32,256]{1,0:T(8,128)S(1)} %get-tuple-element.19), channel_id=1, source_target_pairs={{0,64},{16,80},{32,96},{48,112},{64,0},{80,16},{96,32},{112,48},{1... | collective-permute-start | bytes 98312 | tf_op jit(solution)/shard_map/ppermute | solution.py:313
  64.3 1.3 %collective-permute-start.3 = (f32[32,256]{1,0:T(8,128)S(1)}, f32[32,256]{1,0:T(8,128)S(1)}, u32[]{:S(2)}, u32[]{:S(2)}) collective-permute-start(f32[32,256]{1,0:T(8,128)S(1)} %get-tuple-element.20), channel_id=1, source_target_pairs={{0,96},{16,112},{32,0},{48,16},{64,32},{80,48},{96,64},{112,80},{1... | collective-permute-start | bytes 98312 | tf_op jit(solution)/shard_map/ppermute | solution.py:313
  65.7 0.0 collective-permute-done.1
  65.7 1.2 %collective-permute-done.2 = f32[32,256]{1,0:T(8,128)S(1)} collective-permute-done((f32[32,256]{1,0:T(8,128)S(1)}, f32[32,256]{1,0:T(8,128)S(1)}, u32[]{:S(2)}, u32[]{:S(2)}) %collective-permute-start.2) | collective-permute-done | bytes 32800 | tf_op jit(solution)/shard_map/ppermute | solution.py:313
  66.8 1.4 %collective-permute-done.3 = f32[32,256]{1,0:T(8,128)S(1)} collective-permute-done((f32[32,256]{1,0:T(8,128)S(1)}, f32[32,256]{1,0:T(8,128)S(1)}, u32[]{:S(2)}, u32[]{:S(2)}) %collective-permute-start.3) | collective-permute-done | bytes 32800 | tf_op jit(solution)/shard_map/ppermute | solution.py:313
  68.2 0.6 add_convert_fusion
  68.9 2.4 %all-to-all-done.1.delta = f32[16,128,128]{2,1,0:T(8,128)S(1)} async-done(((f32[16,128,128]{2,1,0:T(8,128)}), f32[16,128,128]{2,1,0:T(8,128)S(1)}, u32[]{:S(2)}, u32[]{:S(2)}) %all-to-all-start.1) | async-done | bytes 1048608 | tf_op jit(solution)/shard_map/all_to_all | solution.py:401
  71.2 8.1 %update_state.1 = f32[512,4,8,128]{3,2,1,0:T(8,128)} custom-call(f32[16,128,128]{2,1,0:T(8,128)S(1)} %all-to-all-done.1.delta, f32[16,512]{1,0:T(8,128)} %get-tuple-element.22.keys_hbm, f32[512,4]{1,0:T(8,128)} %get-tuple-element.23.decay_hbm, f32[512,4,8,128]{3,2,1,0:T(8,128)} %state_hbm.3), custom_call_target="tpu_custom_call" | custom-call | tf_op jit(solution)/shard_map/update_state/pallas_call | solution.py:405
  (3 shorter events, 0.0 us)
Async XLA Ops:
  0.6 17.6 %copy-start = (bf16[2048,4,128]{2,1,0:T(4,128)(2,1)S(1)}, bf16[2048,4,128]{2,1,0:T(4,128)(2,1)}, u32[]{:S(2)}) copy-start(bf16[2048,4,128]{2,1,0:T(4,128)(2,1)} %param.15) | copy-start | bytes 6291460
  10.2 39.3 %all-to-all-start = ((f32[16,264,128]{2,1,0:T(8,128)}), f32[16,264,128]{2,1,0:T(8,128)}, u32[]{:S(2)}, u32[]{:S(2)}) async-start(f32[16,264,128]{2,1,0:T(8,128)} %get-tuple-element.13), calls=%async_computation | async-start | bytes 4325376 | tf_op jit(solution)/shard_map/all_to_all | solution.py:383
  18.3 1.7 %copy-start.6 = (bf16[2048,4,128]{2,1,0:T(4,128)(2,1)S(1)}, bf16[2048,4,128]{2,1,0:T(4,128)(2,1)}, u32[]{:S(2)}) copy-start(bf16[2048,4,128]{2,1,0:T(4,128)(2,1)} %param.16) | copy-start | bytes 6291460
  18.3 3.0 %copy-start.4 = (f32[4]{0:T(128)S(1)}, f32[4]{0:T(128)}, u32[]{:S(2)}) copy-start(f32[4]{0:T(128)} %param.19) | copy-start | bytes 52
  18.3 3.0 %copy-start.7 = (bf16[2048,4]{0,1:T(4,128)(2,1)S(1)}, bf16[2048,4]{0,1:T(4,128)(2,1)}, u32[]{:S(2)}) copy-start(bf16[2048,4]{0,1:T(4,128)(2,1)} %param.18) | copy-start | bytes 49156
  18.3 4.1 %copy-start.3 = (bf16[2048,4]{0,1:T(4,128)(2,1)S(1)}, bf16[2048,4]{0,1:T(4,128)(2,1)}, u32[]{:S(2)}) copy-start(bf16[2048,4]{0,1:T(4,128)(2,1)} %param.17) | copy-start | bytes 49156
  18.3 4.1 %copy-start.5 = (f32[4]{0:T(128)S(1)}, f32[4]{0:T(128)}, u32[]{:S(2)}) copy-start(f32[4]{0:T(128)} %param.20) | copy-start | bytes 52
  18.3 31.2 %copy-start.2 = (f32[128]{0:T(128)S(1)}, f32[128]{0:T(128)}, u32[]{:S(2)}) copy-start(f32[128]{0:T(128)} %param.21) | copy-start | bytes 1540
  51.6 1.0 %copy-start.1 = (f32[16,128,128]{2,1,0:T(8,128)}, f32[16,128,128]{2,1,0:T(8,128)S(1)}, u32[]{:S(2)}) copy-start(f32[16,128,128]{2,1,0:T(8,128)S(1)} %get-tuple-element.21) | copy-start | bytes 3145732
  52.6 18.7 %all-to-all-start.1 = ((f32[16,128,128]{2,1,0:T(8,128)}), f32[16,128,128]{2,1,0:T(8,128)S(1)}, u32[]{:S(2)}, u32[]{:S(2)}) async-start(f32[16,128,128]{2,1,0:T(8,128)} %copy-done.1), calls=%async_computation.1 | async-start | bytes 2097152 | tf_op jit(solution)/shard_map/all_to_all | solution.py:401
  58.3 1.4 %collective-permute-start = (f32[4,32,256]{2,1,0:T(8,128)S(1)}, f32[4,32,256]{2,1,0:T(8,128)S(1)}, u32[]{:S(2)}, u32[]{:S(2)}) collective-permute-start(f32[4,32,256]{2,1,0:T(8,128)S(1)} %get-tuple-element.16), channel_id=1, source_target_pairs={{0,16},{16,0},{32,48},{48,32},{64,80},{80,64},{96,112},{112,96},{1... | collective-permute-start | bytes 393224 | tf_op jit(solution)/shard_map/ppermute | solution.py:303
  59.8 5.9 %collective-permute-start.1 = (f32[32,256]{1,0:T(8,128)S(1)}, f32[32,256]{1,0:T(8,128)S(1)}, u32[]{:S(2)}, u32[]{:S(2)}) collective-permute-start(f32[32,256]{1,0:T(8,128)S(1)} %get-tuple-element.18), channel_id=1, source_target_pairs={{0,32},{16,48},{32,64},{48,80},{64,96},{80,112},{96,0},{112,16},{1... | collective-permute-start | bytes 98312 | tf_op jit(solution)/shard_map/ppermute | solution.py:313
  61.4 5.4 %collective-permute-start.2 = (f32[32,256]{1,0:T(8,128)S(1)}, f32[32,256]{1,0:T(8,128)S(1)}, u32[]{:S(2)}, u32[]{:S(2)}) collective-permute-start(f32[32,256]{1,0:T(8,128)S(1)} %get-tuple-element.19), channel_id=1, source_target_pairs={{0,64},{16,80},{32,96},{48,112},{64,0},{80,16},{96,32},{112,48},{1... | collective-permute-start | bytes 98312 | tf_op jit(solution)/shard_map/ppermute | solution.py:313
  64.3 3.9 %collective-permute-start.3 = (f32[32,256]{1,0:T(8,128)S(1)}, f32[32,256]{1,0:T(8,128)S(1)}, u32[]{:S(2)}, u32[]{:S(2)}) collective-permute-start(f32[32,256]{1,0:T(8,128)S(1)} %get-tuple-element.20), channel_id=1, source_target_pairs={{0,96},{16,112},{32,0},{48,16},{64,32},{80,48},{96,64},{112,80},{1... | collective-permute-start | bytes 98312 | tf_op jit(solution)/shard_map/ppermute | solution.py:313

commit v4 on v3

--- a/solution.py
+++ b/solution.py
@@ -8,6 +8,8 @@
 
 LANES = 128
 SUB = 8
+BLOCK = 16
+SIDE = 4
 
 
 def high_low(value):
@@ -27,33 +29,22 @@
     decay_log_hbm,
     dt_bias_hbm,
     state_hbm,
-    sent_hbm,
-    keys_hbm,
-    decay_hbm,
-    hidden,
-    weights,
-    w_decay,
-    decay_log,
-    dt_bias,
-    state,
-    sent,
-    picks,
-    sums,
-    keys_all,
-    decay_all,
-    in_sems,
-    hidden_sems,
-    state_sems,
-    sent_sems,
-    out_sems,
+    *rest,
 ):
+    by_x, by_z = rest[0:SIDE], rest[SIDE : 2 * SIDE]
+    keys_hbm, decay_hbm, hidden, weights, w_decay, decay_log, dt_bias, state = rest[2 * SIDE : 2 * SIDE + 8]
+    reads_k, reads_q, left, picks, sums, keys_all, decay_all = rest[2 * SIDE + 8 : 2 * SIDE + 15]
+    in_sems, hidden_sems, state_sems, k_sems, q_sems, out_sems = rest[2 * SIDE + 15 :]
+    me = lax.axis_index("row")
+    my_x, my_z = me // SIDE, me % SIDE
     parts, rows, heads = state.shape[0:3]
     chunks = hidden.shape[0]
-    per_chunk = parts // chunks
+    blocks = LANES // BLOCK
     key_rows = w_query_hbm.shape[0]
     key_heads = key_rows // SUB
     group = heads // key_heads
-    span = rows * SUB
+    few = BLOCK
+    span = few * SUB
     pad = weights.dtype.itemsize * SUB
 
     inputs = [
@@ -66,14 +57,22 @@
     for copy in inputs:
         copy.start()
 
-    def hidden_copy(n):
-        return pltpu.make_async_copy(hidden_hbm.at[pl.ds(n * LANES, LANES)], hidden.at[n], hidden_sems.at[n])
+    def chunk_of(s):
+        return (my_x + s) % SIDE
+
+    def hidden_copy(s):
+        at = pl.multiple_of(chunk_of(s) * LANES, LANES)
+        return pltpu.make_async_copy(hidden_hbm.at[pl.ds(at, LANES)], hidden.at[s], hidden_sems.at[s])
 
     def state_copy(n):
-        return pltpu.make_async_copy(state_hbm.at[pl.ds(n * rows, rows)], state.at[n], state_sems.at[n])
-
-    def sent_copy(n):
-        return pltpu.make_async_copy(sent.at[n], sent_hbm.at[n], sent_sems.at[n])
+        part = chunk_of(n // SIDE) * SIDE + (my_z + n % SIDE) % SIDE
+        return pltpu.make_async_copy(state_hbm.at[pl.ds(part * rows, rows)], state.at[n], state_sems.at[n])
+
+    def k_copy(s, to):
+        return pltpu.make_async_copy(reads_k.at[s], to, k_sems.at[s])
+
+    def q_copy(s, t):
+        return pltpu.make_async_copy(reads_q.at[s, t], by_z[t].at[s], q_sems.at[s, t])
 
     ahead = 8
     for n in range(chunks):
@@ -84,7 +83,7 @@
     sums[...] = jnp.zeros(sums.shape, sums.dtype)
     source = lax.broadcasted_iota(jnp.int32, (LANES, span), 0)
     entry = lax.broadcasted_iota(jnp.int32, (LANES, span), 1) % SUB
-    own = lax.broadcasted_iota(jnp.int32, (rows, span), 1) // SUB == lax.broadcasted_iota(jnp.int32, (rows, span), 0)
+    own = lax.broadcasted_iota(jnp.int32, (few, span), 1) // SUB == lax.broadcasted_iota(jnp.int32, (few, span), 0)
     for n in range(2 * key_heads):
         picks[n] = (source == pad + n * SUB + entry).astype(jnp.bfloat16)
     for copy in inputs:
@@ -92,20 +91,20 @@
     weights[0:heads] = w_decay[...]
 
     @pl.loop(0, chunks)
-    def _(chunk):
-        hidden_copy(chunk).wait()
-
-        @pl.when(chunk == 0)
+    def _(s):
+        chunk = chunk_of(s)
+        hidden_copy(s).wait()
+
+        @pl.when(s == 0)
         def _():
             for n in range(ahead):
                 state_copy(n).start()
 
-        projected = lax.dot_general(hidden[chunk], weights[...], (((1,), (1,)), ((), ())), preferred_element_type=jnp.float32)
+        projected = lax.dot_general(hidden[s], weights[...], (((1,), (1,)), ((), ())), preferred_element_type=jnp.float32)
         halves = jnp.concatenate(high_low(projected), axis=0)
-        left = []
         for n in range(2 * key_heads):
-            wide = dot(halves, picks[n]).reshape(2 * per_chunk, rows, span)
-            left.append(jnp.where(own[None], wide, 0.0).astype(jnp.bfloat16))
+            wide = dot(halves, picks[n]).reshape(2 * blocks, few, span)
+            left[n] = jnp.where(own[None], wide, 0.0).astype(jnp.bfloat16)
 
         at = pl.multiple_of(chunk * LANES, LANES)
         pre = projected[:, 0:heads] + dt_bias[...]
@@ -119,30 +118,36 @@
             for g in range(key_heads):
                 sums[n * key_heads + g : n * key_heads + g + 1] = jnp.sum(product[g * SUB : (g + 1) * SUB], axis=0, keepdims=True)
 
-        for p in range(per_chunk):
-            part = chunk * per_chunk + p
-            state_copy(part).wait()
-
-            @pl.when(part + ahead < parts)
+        for t in range(SIDE):
+            p = (my_z + t) % SIDE
+            turn = s * SIDE + t
+            state_copy(turn).wait()
+
+            @pl.when(turn + ahead < parts)
             def _():
-                state_copy(part + ahead).start()
-
-            for g in range(key_heads):
-                tiles = [state[part, :, g * group + j].reshape(span, LANES) for j in range(group)]
-                state_high, state_low = high_low(jnp.concatenate(tiles, axis=1))
-                q_left, k_left = left[g], left[key_heads + g]
-                high = jnp.concatenate([q_left[p], k_left[p]], axis=0)
-                both = dot(jnp.concatenate([high, q_left[per_chunk + p], k_left[per_chunk + p]], axis=0), state_high)
-                read = both[0 : 2 * rows] + both[2 * rows :] + dot(high, state_low)
-                for j in range(group):
-                    to = (g * group + j) * rows
-                    lanes = slice(j * LANES, (j + 1) * LANES)
-                    sent[part, to : to + rows] = read[rows:, lanes]
-                    to += heads * rows
-                    sent[part, to : to + rows] = read[0:rows, lanes]
-            to = 2 * heads * rows
-            sent[part, to : to + SUB] = pltpu.roll(sums[...], (LANES - p * rows) % LANES, 1)
-            sent_copy(part).start()
+                state_copy(turn + ahead).start()
+
+            for first in range(0, rows, few):
+                block = p * (rows // few) + first // few
+                for g in range(key_heads):
+                    tiles = [state[turn, first : first + few, g * group + j].reshape(span, LANES) for j in range(group)]
+                    state_high, state_low = high_low(jnp.concatenate(tiles, axis=1))
+                    high = jnp.concatenate([left[g, block], left[key_heads + g, block]], axis=0)
+                    low = jnp.concatenate([left[g, blocks + block], left[key_heads + g, blocks + block]], axis=0)
+                    both = dot(jnp.concatenate([high, low], axis=0), state_high)
+                    read = both[0 : 2 * few] + both[2 * few :] + dot(high, state_low)
+                    for j in range(group):
+                        to = (g * group + j) * rows + first
+                        lanes = slice(j * LANES, (j + 1) * LANES)
+                        reads_k[s, t, to : to + few] = read[few:, lanes]
+                        reads_q[s, t, to : to + few] = read[0:few, lanes]
+            reads_q[s, t, heads * rows :] = pltpu.roll(sums[...], (LANES - p * rows) % LANES, 1)
+            q_copy(s, t).start()
+        for k in range(SIDE):
+
+            @pl.when(s == k)
+            def _():
+                k_copy(s, by_x[k]).start()
 
     outputs = [
         pltpu.make_async_copy(keys_all, keys_hbm, out_sems.at[0]),
@@ -151,50 +156,57 @@
     for copy in outputs:
         copy.start()
 
-    @pl.loop(0, parts)
-    def _(part):
-        sent_copy(part).wait()
-
+    for k in range(SIDE):
+        k_copy(k, by_x[k]).wait()
+        for t in range(SIDE):
+            q_copy(k, t).wait()
     for copy in outputs:
         copy.wait()
 
 
-def owner_kernel(arrived, values, zgate, decay, beta, norm_gain, delta_out, normed_out):
+def owner_kernel(*refs):
+    arrived = refs[0 : 2 * SIDE]
+    values, zgate, decay, beta, norm_gain, delta_hbm, normed_out, scaled, out_sems = refs[2 * SIDE :]
     rows, heads = decay.shape
+    parts = delta_hbm.shape[0]
     key_heads = 2
     group = heads // key_heads
-    total = arrived[0]
-    for n in range(1, arrived.shape[0]):
-        total = total + arrived[n]
-    sums = jnp.transpose(total[2 * heads * rows :])[0:rows]
+    read_k, read_q = ((x[0][...] + x[1][...]) + (x[2][...] + x[3][...]) for x in (arrived[0:SIDE], arrived[SIDE:]))
+    sums = jnp.transpose(read_q[heads * rows :])[0:rows]
     query_scale = lax.rsqrt(1.0 + sums[:, 0:key_heads])
     key_scale = lax.rsqrt(1.0 + sums[:, key_heads : 2 * key_heads])
     unit_dot = sums[:, 2 * key_heads : 3 * key_heads] * query_scale * key_scale
+    reads = []
     for h in range(heads):
         g = h // group
         lanes = slice(h * LANES, (h + 1) * LANES)
         d = decay[:, h : h + 1]
         ks = key_scale[:, g : g + 1]
-        readk = total[h * rows : (h + 1) * rows] * ks
+        readk = read_k[h * rows : (h + 1) * rows] * ks
         delta = beta[:, h : h + 1] * (values[:, lanes] - d * readk)
-        raw_q = total[(heads + h) * rows : (heads + h + 1) * rows]
-        readq = d * (raw_q * query_scale[:, g : g + 1]) + unit_dot[:, g : g + 1] * delta
+        raw_q = read_q[h * rows : (h + 1) * rows]
+        scaled[h * rows : (h + 1) * rows] = delta * ks
+        reads.append(d * (raw_q * query_scale[:, g : g + 1]) + unit_dot[:, g : g + 1] * delta)
+    outputs = [pltpu.make_async_copy(scaled, delta_hbm.at[n], out_sems.at[n]) for n in range(parts)]
+    for copy in outputs:
+        copy.start()
+    for h, readq in enumerate(reads):
+        lanes = slice(h * LANES, (h + 1) * LANES)
         meansq = jnp.mean(readq * readq, axis=1, keepdims=True)
         z = zgate[:, lanes]
         normed = readq * lax.rsqrt(meansq + 0.5) * norm_gain[...] * (z / (1.0 + jnp.exp(-z)))
         normed_out[:, lanes] = normed.astype(jnp.bfloat16)
-        scaled = delta * ks
-        for n in range(delta_out.shape[0]):
-            delta_out[n, h * rows : (h + 1) * rows] = scaled
+    for copy in outputs:
+        copy.wait()
 
 
 def update_kernel(delta, keys_hbm, decay_hbm, state_hbm, new_state, keys, decay, wide, state, ready, small_sems, in_sems, out_sems):
     parts, rows, heads = state.shape[0:3]
     key_heads = keys.shape[0] // SUB
     group = heads // key_heads
-    span = rows * SUB
+    few = BLOCK
+    span = few * SUB
     per_tile = LANES // rows
-    together = 4
 
     small = [
         pltpu.make_async_copy(decay_hbm, decay, small_sems.at[0]),
@@ -214,7 +226,7 @@
         read(n).start()
     lane = lax.broadcasted_iota(jnp.int32, (SUB, LANES), 1)
     slot = lax.broadcasted_iota(jnp.int32, (span, LANES), 1)
-    own = (slot % rows == lax.broadcasted_iota(jnp.int32, (span, LANES), 0) // SUB) & (slot < 3 * rows)
+    own = (slot % few == lax.broadcasted_iota(jnp.int32, (span, LANES), 0) // SUB) & (slot < 3 * few)
     ones = jnp.ones((LANES, LANES), jnp.bfloat16)
     for copy in small:
         copy.wait()
@@ -227,32 +239,35 @@
             spread = jnp.broadcast_to(some[:, h : h + 1], (LANES, LANES)).reshape(per_tile, rows, LANES)
             wide[pl.ds(n * per_tile, per_tile), :, h * LANES : (h + 1) * LANES] = spread
 
-    @pl.loop(0, parts // together)
-    def _(pair):
-        tile = keys[:, pl.ds(pl.multiple_of(pair * together // per_tile * LANES, LANES), LANES)]
-        for n in range(together):
-            part = pair * together + n
-            key = pltpu.roll(tile, (LANES - part % per_tile * rows) % LANES, 1)
-            high = key.astype(jnp.bfloat16).astype(jnp.float32)
-            rest = key - high
-            middle = rest.astype(jnp.bfloat16).astype(jnp.float32)
-            low = pltpu.roll(rest - middle, 2 * rows, 1)
-            packed = jnp.where(lane[0:1] < rows, high, jnp.where(lane[0:1] < 2 * rows, pltpu.roll(middle, rows, 1), low))
+    @pl.loop(0, parts // per_tile)
+    def _(tile):
+        raw = keys[:, pl.ds(pl.multiple_of(tile * LANES, LANES), LANES)]
+        high = raw.astype(jnp.bfloat16).astype(jnp.float32)
+        rest = raw - high
+        middle = rest.astype(jnp.bfloat16).astype(jnp.float32)
+        low = rest - middle
+        for n in range(per_tile):
+            part = tile * per_tile + n
             read(part).wait()
 
             @pl.when(part + ahead < parts)
             def _():
                 read(part + ahead).start()
 
-            for g in range(key_heads):
-                spread = jnp.broadcast_to(packed[None, g * SUB : (g + 1) * SUB], (rows, SUB, LANES)).reshape(span, LANES)
-                wide_key = dot(jnp.where(own, spread, 0.0).astype(jnp.bfloat16), ones)
-                for b in range(rows):
-                    k = wide_key[b * SUB : (b + 1) * SUB]
-                    for h in range(g * group, (g + 1) * group):
-                        row = jnp.broadcast_to(delta[part, h * rows + b : h * rows + b + 1], (SUB, LANES))
-                        factor = jnp.broadcast_to(wide[part, b : b + 1, h * LANES : (h + 1) * LANES], (SUB, LANES))
-                        ready[part, b, h] = factor * state[part, b, h] + k * row
+            for first in range(0, rows, few):
+                back = LANES - n * rows - first
+                turned = [pltpu.roll(x, (back + m * few) % LANES, 1) for m, x in enumerate((high, middle, low))]
+                packed = jnp.where(lane[0:1] < few, turned[0], jnp.where(lane[0:1] < 2 * few, turned[1], turned[2]))
+                for g in range(key_heads):
+                    spread = jnp.broadcast_to(packed[None, g * SUB : (g + 1) * SUB], (few, SUB, LANES)).reshape(span, LANES)
+                    wide_key = dot(jnp.where(own, spread, 0.0).astype(jnp.bfloat16), ones)
+                    for b in range(few):
+                        k = wide_key[b * SUB : (b + 1) * SUB]
+                        at = first + b
+                        for h in range(g * group, (g + 1) * group):
+                            row = jnp.broadcast_to(delta[part, h * rows + at : h * rows + at + 1], (SUB, LANES))
+                            factor = jnp.broadcast_to(wide[part, at : at + 1, h * LANES : (h + 1) * LANES], (SUB, LANES))
+                            ready[part, at, h] = factor * state[part, at, h] + k * row
             write(part).start()
 
     @pl.loop(0, parts)
@@ -333,7 +348,6 @@
     rows = seqs // parts
     heads = state.shape[1]
     key_rows = w_query.shape[1] * w_query.shape[2]
-    per_part = 2 * heads * rows + SUB
     f32 = jnp.float32
 
     def in_hbm(value):
@@ -342,15 +356,15 @@
     any_space = pl.BlockSpec(memory_space=pl.ANY)
     in_vmem = pl.BlockSpec(memory_space=pltpu.VMEM)
     limit = pltpu.CompilerParams(vmem_limit_bytes=20 * 1024 * 1024)
-    sent, keys, decay_all = pl.pallas_call(
+    extra = heads * rows + SUB
+    per_k, per_q = (SIDE, heads * rows, LANES), (SIDE, extra, LANES)
+    *sent, keys, decay_all = pl.pallas_call(
         read_kernel,
         in_specs=[any_space] * 7,
-        out_specs=[any_space] * 3,
-        out_shape=[
-            pltpu.HBM((parts, per_part, LANES), f32),
-            pltpu.HBM((key_rows, seqs), f32),
-            pltpu.HBM((seqs, heads), f32),
-        ],
+        out_specs=[in_vmem] * (2 * SIDE) + [any_space] * 2,
+        out_shape=[pltpu.VMEM(per_k, f32)] * SIDE
+        + [pltpu.VMEM(per_q, f32)] * SIDE
+        + [pltpu.HBM((key_rows, seqs), f32), pltpu.HBM((seqs, heads), f32)],
         scratch_shapes=[
             pltpu.VMEM((seqs // LANES, LANES, width), jnp.bfloat16),
             pltpu.VMEM((LANES, width), jnp.bfloat16),
@@ -358,15 +372,18 @@
             pltpu.VMEM((1, heads), f32),
             pltpu.VMEM((1, heads), f32),
             pltpu.VMEM((parts, rows, heads, SUB, LANES), f32),
-            pltpu.VMEM((parts, per_part, LANES), f32),
-            pltpu.VMEM((2 * key_rows // SUB, LANES, rows * SUB), jnp.bfloat16),
+            pltpu.VMEM((SIDE, *per_k), f32),
+            pltpu.VMEM((SIDE, *per_q), f32),
+            pltpu.VMEM((2 * key_rows // SUB, 2 * LANES // BLOCK, BLOCK, BLOCK * SUB), jnp.bfloat16),
+            pltpu.VMEM((2 * key_rows // SUB, LANES, BLOCK * SUB), jnp.bfloat16),
             pltpu.VMEM((SUB, LANES), f32),
             pltpu.VMEM((key_rows, seqs), f32),
             pltpu.VMEM((seqs, heads), f32),
             pltpu.SemaphoreType.DMA((5,)),
             pltpu.SemaphoreType.DMA((seqs // LANES,)),
             pltpu.SemaphoreType.DMA((parts,)),
-            pltpu.SemaphoreType.DMA((parts,)),
+            pltpu.SemaphoreType.DMA((SIDE,)),
+            pltpu.SemaphoreType.DMA((SIDE, SIDE)),
             pltpu.SemaphoreType.DMA((2,)),
         ],
         compiler_params=limit,
@@ -380,7 +397,22 @@
         in_hbm(dt_bias[None]),
         in_hbm(state),
     )
-    arrived = lax.all_to_all(sent, "row", 0, 0, tiled=True)
+
+    def along_x(value, step):
+        return lax.ppermute(value, "row", [(n, (n + SIDE * step) % parts) for n in range(parts)])
+
+    def along_z(value, step):
+        return lax.ppermute(value, "row", [(n, n // SIDE * SIDE + (n + step) % SIDE) for n in range(parts)])
+
+    steps = (1, 3, 2)
+    got_k = [along_x(sent[n], n) for n in steps]
+    got_q = [along_z(sent[SIDE + n], n) for n in steps]
+    part_k, part_q = (
+        [(own[n] + got[0][n]) + (got[1][n] + got[2][n]) for n in range(SIDE)]
+        for own, got in ((sent[0], got_k), (sent[SIDE], got_q))
+    )
+    arrived = [part_k[0], *(along_z(part_k[n], n) for n in steps)]
+    arrived += [part_q[0], *(along_x(part_q[n], n) for n in steps)]
 
     own_hidden = lax.dynamic_slice_in_dim(hidden_in, lax.axis_index("row") * rows, rows, 0)
     values = jnp.einsum("bd,dhv->bhv", own_hidden, w_value, preferred_element_type=f32).reshape(rows, heads * LANES)
@@ -391,13 +423,19 @@
 
     delta_own, normed = pl.pallas_call(
         owner_kernel,
+        in_specs=[in_vmem] * (2 * SIDE + 5),
+        out_specs=[any_space, in_vmem],
         out_shape=[
-            pltpu.VMEM((parts, heads * rows, LANES), f32),
+            pltpu.HBM((parts, heads * rows, LANES), f32),
             pltpu.VMEM((rows, heads * LANES), jnp.bfloat16),
+        ],
+        scratch_shapes=[
+            pltpu.VMEM((heads * rows, LANES), f32),
+            pltpu.SemaphoreType.DMA((parts,)),
         ],
         compiler_params=limit,
         name="owner_rows",
-    )(arrived, values, zgate, decay, beta, norm_gain[None])
+    )(*arrived, values, zgate, decay, beta, norm_gain[None])
     delta = lax.all_to_all(delta_own, "row", 0, 0, tiled=True)
 
     layer_out = head_exchange(normed, w_out.reshape(heads * LANES, -1), lax.axis_size("head") // 2).astype(jnp.bfloat16)

time: 79.8 us -> 74.5 us (0.934)
  waiting for transfers between devices: 32.3 us -> 11 us
  starting transfers between devices: 17.7 us -> 30.7 us
  other arithmetic: 0.62 us -> 3.01 us
  Pallas kernels: 21.8 us -> 23.2 us
  local copies, waits for them, and re-layouts: 1.1 us -> 0.17 us
    all_to_all x1 -> x0, waiting for transfers between devices: 26 us -> none  [decode(): arrived = lax.all_to_all(sent, 'row', 0, 0, tiled=True)]
    ppermute x0 -> x12, starting transfers between devices: none -> 21.1 us  [the longest x6 12 us: along_z(): lax.ppermute(value, 'row', [(n, n // SIDE * SIDE + (n + step) % SIDE) for...]
    all_to_all x1 -> x0, starting transfers between devices: 8.05 us -> none  [decode(): arrived = lax.all_to_all(sent, 'row', 0, 0, tiled=True)]
    ppermute x0 -> x12, waiting for transfers between devices: none -> 5.36 us  [the longest x6 5.35 us: along_x(): lax.ppermute(value, 'row', [(n, (n + SIDE * step) % parts) for n in range...]
    add x0 -> x2, other arithmetic: none -> 2.39 us  [decode(): own[n] + got[0][n] + (got[1][n] + got[2][n])]
    pallas_call x2, Pallas kernels: 11.6 us -> 13 us  [the longest x1 11.6 us: decode(): pl.pallas_call(read_kernel, in_specs=[any_space] * 7, out_specs=[in_vmem]...]
    unnamed x16 -> x14, local copies, waits for them, and re-layouts: 1.09 us -> 0.16 us
  transfers between devices with their start and end apart: 6 -> 17, of which waited for: 5 -> 7; matrix products, arithmetic and copies ran while one was open for 7% -> 11% of each run, Pallas kernels for 3% -> 3%
where the time goes in v4:
time: 74.5 us; the launch traced here: 74 us
  starting transfers between devices  30.7 us (41%)
  Pallas kernels  23.2 us (31%)
  waiting for transfers between devices  11 us (15%)
  matrix products  5.05 us (7%)
  other arithmetic  3.01 us (4%)
  between operations  0.82 us (1%)
    ppermute x6, starting transfers between devices, along_z(): lax.ppermute(value, 'row', [(n, n // SIDE * SIDE + (n + step) % SIDE) for...  12 us
    pallas_call x1, Pallas kernels, decode(): pl.pallas_call(read_kernel, in_specs=[any_space] * 7, out_specs=[in_vmem]...  11.6 us
    ppermute x6, starting transfers between devices, along_x(): lax.ppermute(value, 'row', [(n, (n + SIDE * step) % parts) for n in range...  9.13 us
    pallas_call x1, Pallas kernels, decode(): pl.pallas_call(update_kernel, in_specs=[in_vmem, any_space, any_space, an...  8.11 us
    ppermute x3, starting transfers between devices, head_exchange(): lax.ppermute(part, 'head', [(h, (h + 2 * s) % heads) for h in range(heads)])  5.89 us
    ppermute x6, waiting for transfers between devices, along_x(): lax.ppermute(value, 'row', [(n, (n + SIDE * step) % parts) for n in range...  5.35 us
    all_to_all x1, starting transfers between devices, decode(): delta = lax.all_to_all(delta_own, 'row', 0, 0, tiled=True)  3.67 us
    ppermute x3, waiting for transfers between devices, head_exchange(): lax.ppermute(part, 'head', [(h, (h + 2 * s) % heads) for h in range(heads)])  2.56 us
  transfers between devices with their start and end apart: 17, of which 7 were waited for; matrix products, arithmetic and copies ran while one was open for 11% of the time, Pallas kernels for 3%

profile of v4, /device:TPU:0, one launch (start us, length us, event | category | flops | bytes accessed | tf_op | source)
XLA Modules:
  0.0 74.0 jit_solution(16243571446969608478)
XLA Ops:
  0.6 0.0 copy-start
  0.6 11.6 %read_state.1 = (f32[4,128,128]{2,1,0:T(8,128)S(1)}, f32[4,128,128]{2,1,0:T(8,128)}, f32[4,128,128]{2,1,0:T(8,128)}, f32[4,128,128]{2,1,0:T(8,128)}, f32[4,136,1...) custom-call(bf16[512,2048]{1,0:T(8,128)(2,1)} %hidden_hbm.1, ...), custom_call_target="tpu_custom_call" | custom-call | tf_op jit(solution)/shard_map/read_state/pallas_call | solution.py:361
  12.3 1.7 %collective-permute-start = (f32[4,128,128]{2,1,0:T(8,128)}, f32[4,128,128]{2,1,0:T(8,128)}, u32[]{:S(2)}, u32[]{:S(2)}) collective-permute-start(f32[4,128,128]{2,1,0:T(8,128)} %get-tuple-element.21), channel_id=1, source_target_pairs={{0,4},{1,5},{2,6},{3,7},{4,8},{5,9},{6,10},{7,11},{8,12},{9,13},{1... | collective-permute-start | bytes 786440 | tf_op jit(solution)/shard_map/ppermute | solution.py:402
  14.0 1.6 %collective-permute-start.1 = (f32[4,128,128]{2,1,0:T(8,128)}, f32[4,128,128]{2,1,0:T(8,128)}, u32[]{:S(2)}, u32[]{:S(2)}) collective-permute-start(f32[4,128,128]{2,1,0:T(8,128)} %get-tuple-element.22), channel_id=1, source_target_pairs={{0,12},{1,13},{2,14},{3,15},{4,0},{5,1},{6,2},{7,3},{8,4},{9,5},{1... | collective-permute-start | bytes 786440 | tf_op jit(solution)/shard_map/ppermute | solution.py:402
  15.6 1.9 %collective-permute-start.2 = (f32[4,128,128]{2,1,0:T(8,128)}, f32[4,128,128]{2,1,0:T(8,128)}, u32[]{:S(2)}, u32[]{:S(2)}) collective-permute-start(f32[4,128,128]{2,1,0:T(8,128)} %get-tuple-element.23), channel_id=1, source_target_pairs={{0,8},{1,9},{2,10},{3,11},{4,12},{5,13},{6,14},{7,15},{8,0},{9,1},... | collective-permute-start | bytes 786440 | tf_op jit(solution)/shard_map/ppermute | solution.py:402
  17.5 1.9 %collective-permute-start.6 = (f32[4,136,128]{2,1,0:T(8,128)S(1)}, f32[4,136,128]{2,1,0:T(8,128)}, u32[]{:S(2)}, u32[]{:S(2)}) collective-permute-start(f32[4,136,128]{2,1,0:T(8,128)S(1)} %get-tuple-element.25), channel_id=1, source_target_pairs={{0,1},{1,2},{2,3},{3,0},{4,5},{5,6},{6,7},{7,4},{8,9},{9,10},{10,1... | collective-permute-start | bytes 835592 | tf_op jit(solution)/shard_map/ppermute | solution.py:405
  19.4 2.1 %collective-permute-start.7 = (f32[4,136,128]{2,1,0:T(8,128)S(1)}, f32[4,136,128]{2,1,0:T(8,128)}, u32[]{:S(2)}, u32[]{:S(2)}) collective-permute-start(f32[4,136,128]{2,1,0:T(8,128)S(1)} %get-tuple-element.26), channel_id=1, source_target_pairs={{0,3},{1,0},{2,1},{3,2},{4,7},{5,4},{6,5},{7,6},{8,11},{9,8},{10,9... | collective-permute-start | bytes 835592 | tf_op jit(solution)/shard_map/ppermute | solution.py:405
  21.6 0.0 copy-done
  21.6 0.0 copy-start.5
  21.6 0.0 copy-start.3
  21.6 0.0 copy-start.2
  21.6 0.0 copy-start.4
  21.6 1.5 %fusion.4 = f32[4,4,8,128]{3,2,1,0:T(8,128)S(1)} fusion(bf16[2048,4,128]{2,1,0:T(4,128)(2,1)S(1)} %copy-done, bf16[512,2048]{1,0:T(8,128)(2,1)} %hidden_hbm.1, s32[]{:T(128)S(6)} %select_n.20), kind=kOutput, calls=%fused_computation.4 | convolution fusion | flops 67108864 | bytes 2293764 | tf_op jit(solution)/shard_map/bd,dhv->bhv/dot_general | solution.py:418
  23.1 0.1 copy-done.5
  23.2 1.4 %fusion.7 = f32[4,4,8,128]{3,2,1,0:T(8,128)S(1)} fusion(bf16[2048,4,128]{2,1,0:T(4,128)(2,1)S(1)} %copy-done.5, bf16[512,2048]{1,0:T(8,128)(2,1)} %hidden_hbm.1, s32[]{:T(128)S(6)} %select_n.20), kind=kOutput, calls=%fused_computation.5 | convolution fusion | flops 67108864 | bytes 2293764 | tf_op jit(solution)/shard_map/bd,dhv->bhv/dot_general | solution.py:419
  24.6 0.0 copy-start.6
  24.6 0.0 copy-start.1
  24.6 0.0 copy-done.3
  24.6 0.0 collective-permute-done
  24.7 1.9 %collective-permute-start.8 = (f32[4,136,128]{2,1,0:T(8,128)S(1)}, f32[4,136,128]{2,1,0:T(8,128)S(1)}, u32[]{:S(2)}, u32[]{:S(2)}) collective-permute-start(f32[4,136,128]{2,1,0:T(8,128)S(1)} %get-tuple-element.27), channel_id=1, source_target_pairs={{0,2},{1,3},{2,0},{3,1},{4,6},{5,7},{6,4},{7,5},{8,10},{9,11},{10,... | collective-permute-start | bytes 835592 | tf_op jit(solution)/shard_map/ppermute | solution.py:405
  26.6 0.0 copy-done.2
  26.6 0.0 copy-done.4
  26.6 1.1 %fusion.36.refs_10_ = f32[32,4]{1,0:T(8,128)S(1)} fusion(bf16[2048,4]{0,1:T(4,128)(2,1)S(1)} %copy-done.2, bf16[512,2048]{1,0:T(8,128)(2,1)} %hidden_hbm.1, s32[]{:T(128)S(6)} %select_n.20, f32[4]{0:T(128)S(1)} %copy-done.4, f32[4]{0:T(128)S(1)} %exponential_negate_fusion), kind=kOutput, calls=%fused_computation.54 | convolution fusion | flops 525312 | bytes 148004 | tf_op jit(solution)/shard_map/dot_general | solution.py:420
  27.7 0.0 collective-permute-done.1
  27.7 0.9 %collective-permute-done.2 = f32[4,128,128]{2,1,0:T(8,128)} collective-permute-done((f32[4,128,128]{2,1,0:T(8,128)}, f32[4,128,128]{2,1,0:T(8,128)}, u32[]{:S(2)}, u32[]{:S(2)}) %collective-permute-start.2) | collective-permute-done | bytes 262176 | tf_op jit(solution)/shard_map/ppermute | solution.py:402
  28.6 1.2 %fusion.28 = (f32[128,128]{1,0:T(8,128)S(1)}, f32[128,128]{1,0:T(8,128)S(1)}, f32[128,128]{1,0:T(8,128)S(1)}, f32[128,128]{1,0:T(8,128)S(1)}) fusion(f32[4,128,128]{2,1,0:T(8,128)} %collective-permute-done.2, f32[4,128,128]{2,1,0:T(8,128)} %collective-permute-done.1, f32[4,128,128]{2,1,0:T(8,128)} %collective-permute-done, ...), kind=kLoop, calls=%fused_computation.37 | loop fusion | flops 196608 | bytes 1310720 | tf_op jit(solution)/shard_map/add | solution.py:411
  29.9 4.0 %collective-permute-start.5 = (f32[128,128]{1,0:T(8,128)S(1)}, f32[128,128]{1,0:T(8,128)S(1)}, u32[]{:S(2)}, u32[]{:S(2)}) collective-permute-start(f32[128,128]{1,0:T(8,128)S(1)} %get-tuple-element.42), channel_id=1, source_target_pairs={{0,2},{1,3},{2,0},{3,1},{4,6},{5,7},{6,4},{7,5},{8,10},{9,11},{10,... | collective-permute-start | bytes 196616 | tf_op jit(solution)/shard_map/ppermute | solution.py:405
  33.8 0.7 collective-permute-start.4
  34.5 0.0 collective-permute-done.6
  34.5 1.3 %collective-permute-start.3 = (f32[128,128]{1,0:T(8,128)S(1)}, f32[128,128]{1,0:T(8,128)S(1)}, u32[]{:S(2)}, u32[]{:S(2)}) collective-permute-start(f32[128,128]{1,0:T(8,128)S(1)} %get-tuple-element.44), channel_id=1, source_target_pairs={{0,1},{1,2},{2,3},{3,0},{4,5},{5,6},{6,7},{7,4},{8,9},{9,10},{10,1... | collective-permute-start | bytes 196616 | tf_op jit(solution)/shard_map/ppermute | solution.py:405
  35.8 0.0 collective-permute-done.7
  35.8 0.0 collective-permute-done.8
  35.9 1.2 %fusion.20 = (f32[136,128]{1,0:T(8,128)S(1)}, f32[136,128]{1,0:T(8,128)S(1)}, f32[136,128]{1,0:T(8,128)S(1)}, f32[136,128]{1,0:T(8,128)S(1)}) fusion(f32[4,136,128]{2,1,0:T(8,128)S(1)} %collective-permute-done.8, f32[4,136,128]{2,1,0:T(8,128)} %collective-permute-done.7, f32[4,136,128]{2,1,0:T(8,128)} %collective-permute-done.6, ...), kind=kLoop, calls=%fused_computation.19 | loop fusion | flops 208896 | bytes 1392640 | tf_op jit(solution)/shard_map/add | solution.py:411
  37.0 1.2 %collective-permute-start.11 = (f32[136,128]{1,0:T(8,128)S(1)}, f32[136,128]{1,0:T(8,128)S(1)}, u32[]{:S(2)}, u32[]{:S(2)}) collective-permute-start(f32[136,128]{1,0:T(8,128)S(1)} %get-tuple-element.38), channel_id=1, source_target_pairs={{0,8},{1,9},{2,10},{3,11},{4,12},{5,13},{6,14},{7,15},{8,0},{9,1},... | collective-permute-start | bytes 208904 | tf_op jit(solution)/shard_map/ppermute | solution.py:402
  38.2 2.7 %collective-permute-start.10 = (f32[136,128]{1,0:T(8,128)S(1)}, f32[136,128]{1,0:T(8,128)S(1)}, u32[]{:S(2)}, u32[]{:S(2)}) collective-permute-start(f32[136,128]{1,0:T(8,128)S(1)} %get-tuple-element.39), channel_id=1, source_target_pairs={{0,12},{1,13},{2,14},{3,15},{4,0},{5,1},{6,2},{7,3},{8,4},{9,5},{1... | collective-permute-start | bytes 208904 | tf_op jit(solution)/shard_map/ppermute | solution.py:402
  40.9 0.0 collective-permute-done.5.refs_3_
  40.9 0.0 collective-permute-start.9
  40.9 0.0 copy-done.6
  40.9 1.1 %fusion.12.refs_11_ = f32[32,4]{1,0:T(8,128)S(1)} fusion(bf16[2048,4]{0,1:T(4,128)(2,1)S(1)} %copy-done.6, bf16[512,2048]{1,0:T(8,128)(2,1)} %hidden_hbm.1, s32[]{:T(128)S(6)} %select_n.20), kind=kOutput, calls=%fused_computation.9 | convolution fusion | flops 524672 | bytes 147972 | tf_op jit(solution)/shard_map/dot_general | solution.py:422
  42.0 0.0 collective-permute-done.4.refs_2_
  42.0 0.0 collective-permute-done.3.refs_1_
  42.1 1.0 %collective-permute-done.11.refs_7_ = f32[136,128]{1,0:T(8,128)S(1)} collective-permute-done((f32[136,128]{1,0:T(8,128)S(1)}, f32[136,128]{1,0:T(8,128)S(1)}, u32[]{:S(2)}, u32[]{:S(2)}) %collective-permute-start.11) | collective-permute-done | bytes 69664 | tf_op jit(solution)/shard_map/ppermute | solution.py:402
  43.0 0.0 collective-permute-done.10.refs_6_
  43.0 3.4 %collective-permute-done.9.refs_5_ = f32[136,128]{1,0:T(8,128)S(1)} collective-permute-done((f32[136,128]{1,0:T(8,128)S(1)}, f32[136,128]{1,0:T(8,128)S(1)}, u32[]{:S(2)}, u32[]{:S(2)}) %collective-permute-start.9) | collective-permute-done | bytes 69664 | tf_op jit(solution)/shard_map/ppermute | solution.py:402
  46.5 0.0 copy-done.1
  46.5 1.3 %owner_rows.1 = (f32[16,128,128]{2,1,0:T(8,128)}, bf16[32,512]{1,0:T(8,128)(2,1)S(1)}) custom-call(f32[128,128]{1,0:T(8,128)S(1)} %get-tuple-element.45.refs_0_, f32[128,128]{1,0:T(8,128)S(1)} %collective-permute-done.3.refs_1_, f32[128,128]{1,0:T(8,128)S(1)} %collective-permute-done.4.refs_2_, f32[128,128]{1,0:T(8,128)S(1)} %collective-permute-done.5.refs_3_, ...), custom_call_target="tpu_custom_call" | custom-call | tf_op jit(solution)/shard_map/owner_rows/pallas_call | solution.py:424
  47.8 3.7 %all-to-all-start = ((f32[16,128,128]{2,1,0:T(8,128)}), f32[16,128,128]{2,1,0:T(8,128)S(1)}, u32[]{:S(2)}, u32[]{:S(2)}) async-start(f32[16,128,128]{2,1,0:T(8,128)} %get-tuple-element.35), calls=%async_computation | async-start | bytes 2097152 | tf_op jit(solution)/shard_map/all_to_all | solution.py:439
  51.5 2.1 %project_out.1 = (f32[4,32,256]{2,1,0:T(8,128)S(1)}, f32[4,32,256]{2,1,0:T(8,128)S(1)}) custom-call(s32[1]{0:T(128)} %bitcast.1.core, bf16[32,512]{1,0:T(8,128)(2,1)S(1)} %get-tuple-element.28.normed, bf16[512,2048]{1,0:T(8,128)(2,1)} %bitcast.45), custom_call_target="tpu_custom_call" | custom-call | tf_op jit(solution)/shard_map/project_out/pallas_call | solution.py:309
  53.6 0.1 collective-permute-start.12
  53.7 1.3 %collective-permute-done.12.got = f32[4,32,256]{2,1,0:T(8,128)S(1)} collective-permute-done((f32[4,32,256]{2,1,0:T(8,128)S(1)}, f32[4,32,256]{2,1,0:T(8,128)S(1)}, u32[]{:S(2)}, u32[]{:S(2)}) %collective-permute-start.12) | collective-permute-done | bytes 131104 | tf_op jit(solution)/shard_map/ppermute | solution.py:318
  55.0 1.6 %collective-permute-start.13 = (f32[32,256]{1,0:T(8,128)S(1)}, f32[32,256]{1,0:T(8,128)S(1)}, u32[]{:S(2)}, u32[]{:S(2)}) collective-permute-start(f32[32,256]{1,0:T(8,128)S(1)} %get-tuple-element.32), channel_id=1, source_target_pairs={{0,32},{16,48},{32,64},{48,80},{64,96},{80,112},{96,0},{112,16},{1... | collective-permute-start | bytes 98312 | tf_op jit(solution)/shard_map/ppermute | solution.py:328
  56.7 2.9 %collective-permute-start.14 = (f32[32,256]{1,0:T(8,128)S(1)}, f32[32,256]{1,0:T(8,128)S(1)}, u32[]{:S(2)}, u32[]{:S(2)}) collective-permute-start(f32[32,256]{1,0:T(8,128)S(1)} %get-tuple-element.33), channel_id=1, source_target_pairs={{0,64},{16,80},{32,96},{48,112},{64,0},{80,16},{96,32},{112,48},{1... | collective-permute-start | bytes 98312 | tf_op jit(solution)/shard_map/ppermute | solution.py:328
  59.6 1.3 %collective-permute-start.15 = (f32[32,256]{1,0:T(8,128)S(1)}, f32[32,256]{1,0:T(8,128)S(1)}, u32[]{:S(2)}, u32[]{:S(2)}) collective-permute-start(f32[32,256]{1,0:T(8,128)S(1)} %get-tuple-element.34), channel_id=1, source_target_pairs={{0,96},{16,112},{32,0},{48,16},{64,32},{80,48},{96,64},{112,80},{1... | collective-permute-start | bytes 98312 | tf_op jit(solution)/shard_map/ppermute | solution.py:328
  60.9 0.0 collective-permute-done.13
  60.9 1.2 %collective-permute-done.14 = f32[32,256]{1,0:T(8,128)S(1)} collective-permute-done((f32[32,256]{1,0:T(8,128)S(1)}, f32[32,256]{1,0:T(8,128)S(1)}, u32[]{:S(2)}, u32[]{:S(2)}) %collective-permute-start.14) | collective-permute-done | bytes 32800 | tf_op jit(solution)/shard_map/ppermute | solution.py:328
  62.1 1.4 %collective-permute-done.15 = f32[32,256]{1,0:T(8,128)S(1)} collective-permute-done((f32[32,256]{1,0:T(8,128)S(1)}, f32[32,256]{1,0:T(8,128)S(1)}, u32[]{:S(2)}, u32[]{:S(2)}) %collective-permute-start.15) | collective-permute-done | bytes 32800 | tf_op jit(solution)/shard_map/ppermute | solution.py:328
  63.5 0.6 add_convert_fusion
  64.1 1.8 %all-to-all-done.delta = f32[16,128,128]{2,1,0:T(8,128)S(1)} async-done(((f32[16,128,128]{2,1,0:T(8,128)}), f32[16,128,128]{2,1,0:T(8,128)S(1)}, u32[]{:S(2)}, u32[]{:S(2)}) %all-to-all-start) | async-done | bytes 1048608 | tf_op jit(solution)/shard_map/all_to_all | solution.py:439
  65.9 8.1 %update_state.1 = f32[512,4,8,128]{3,2,1,0:T(8,128)} custom-call(f32[16,128,128]{2,1,0:T(8,128)S(1)} %all-to-all-done.delta, f32[16,512]{1,0:T(8,128)} %get-tuple-element.36.keys_hbm, f32[512,4]{1,0:T(8,128)} %get-tuple-element.37.decay_hbm, f32[512,4,8,128]{3,2,1,0:T(8,128)} %state_hbm.3), custom_call_target="tpu_custom_call" | custom-call | tf_op jit(solution)/shard_map/update_state/pallas_call | solution.py:443
  (3 shorter events, 0.0 us)
Async XLA Ops:
  0.6 20.9 %copy-start = (bf16[2048,4,128]{2,1,0:T(4,128)(2,1)S(1)}, bf16[2048,4,128]{2,1,0:T(4,128)(2,1)}, u32[]{:S(2)}) copy-start(bf16[2048,4,128]{2,1,0:T(4,128)(2,1)} %param.15) | copy-start | bytes 6291460
  12.3 12.3 %collective-permute-start = (f32[4,128,128]{2,1,0:T(8,128)}, f32[4,128,128]{2,1,0:T(8,128)}, u32[]{:S(2)}, u32[]{:S(2)}) collective-permute-start(f32[4,128,128]{2,1,0:T(8,128)} %get-tuple-element.21), channel_id=1, source_target_pairs={{0,4},{1,5},{2,6},{3,7},{4,8},{5,9},{6,10},{7,11},{8,12},{9,13},{1... | collective-permute-start | bytes 786440 | tf_op jit(solution)/shard_map/ppermute | solution.py:402
  14.0 13.7 %collective-permute-start.1 = (f32[4,128,128]{2,1,0:T(8,128)}, f32[4,128,128]{2,1,0:T(8,128)}, u32[]{:S(2)}, u32[]{:S(2)}) collective-permute-start(f32[4,128,128]{2,1,0:T(8,128)} %get-tuple-element.22), channel_id=1, source_target_pairs={{0,12},{1,13},{2,14},{3,15},{4,0},{5,1},{6,2},{7,3},{8,4},{9,5},{1... | collective-permute-start | bytes 786440 | tf_op jit(solution)/shard_map/ppermute | solution.py:402
  15.6 13.0 %collective-permute-start.2 = (f32[4,128,128]{2,1,0:T(8,128)}, f32[4,128,128]{2,1,0:T(8,128)}, u32[]{:S(2)}, u32[]{:S(2)}) collective-permute-start(f32[4,128,128]{2,1,0:T(8,128)} %get-tuple-element.23), channel_id=1, source_target_pairs={{0,8},{1,9},{2,10},{3,11},{4,12},{5,13},{6,14},{7,15},{8,0},{9,1},... | collective-permute-start | bytes 786440 | tf_op jit(solution)/shard_map/ppermute | solution.py:402
  17.5 17.0 %collective-permute-start.6 = (f32[4,136,128]{2,1,0:T(8,128)S(1)}, f32[4,136,128]{2,1,0:T(8,128)}, u32[]{:S(2)}, u32[]{:S(2)}) collective-permute-start(f32[4,136,128]{2,1,0:T(8,128)S(1)} %get-tuple-element.25), channel_id=1, source_target_pairs={{0,1},{1,2},{2,3},{3,0},{4,5},{5,6},{6,7},{7,4},{8,9},{9,10},{10,1... | collective-permute-start | bytes 835592 | tf_op jit(solution)/shard_map/ppermute | solution.py:405
  19.4 16.4 %collective-permute-start.7 = (f32[4,136,128]{2,1,0:T(8,128)S(1)}, f32[4,136,128]{2,1,0:T(8,128)}, u32[]{:S(2)}, u32[]{:S(2)}) collective-permute-start(f32[4,136,128]{2,1,0:T(8,128)S(1)} %get-tuple-element.26), channel_id=1, source_target_pairs={{0,3},{1,0},{2,1},{3,2},{4,7},{5,4},{6,5},{7,6},{8,11},{9,8},{10,9... | collective-permute-start | bytes 835592 | tf_op jit(solution)/shard_map/ppermute | solution.py:405
  21.6 1.7 %copy-start.5 = (bf16[2048,4,128]{2,1,0:T(4,128)(2,1)S(1)}, bf16[2048,4,128]{2,1,0:T(4,128)(2,1)}, u32[]{:S(2)}) copy-start(bf16[2048,4,128]{2,1,0:T(4,128)(2,1)} %param.16) | copy-start | bytes 6291460
  21.6 3.1 %copy-start.3 = (f32[4]{0:T(128)S(1)}, f32[4]{0:T(128)}, u32[]{:S(2)}) copy-start(f32[4]{0:T(128)} %param.19) | copy-start | bytes 52
  21.6 5.0 %copy-start.2 = (bf16[2048,4]{0,1:T(4,128)(2,1)S(1)}, bf16[2048,4]{0,1:T(4,128)(2,1)}, u32[]{:S(2)}) copy-start(bf16[2048,4]{0,1:T(4,128)(2,1)} %param.17) | copy-start | bytes 49156
  21.6 5.0 %copy-start.4 = (f32[4]{0:T(128)S(1)}, f32[4]{0:T(128)}, u32[]{:S(2)}) copy-start(f32[4]{0:T(128)} %param.20) | copy-start | bytes 52
  24.6 16.4 %copy-start.6 = (bf16[2048,4]{0,1:T(4,128)(2,1)S(1)}, bf16[2048,4]{0,1:T(4,128)(2,1)}, u32[]{:S(2)}) copy-start(bf16[2048,4]{0,1:T(4,128)(2,1)} %param.18) | copy-start | bytes 49156
  24.6 21.9 %copy-start.1 = (f32[128]{0:T(128)S(1)}, f32[128]{0:T(128)}, u32[]{:S(2)}) copy-start(f32[128]{0:T(128)} %param.21) | copy-start | bytes 1540
  24.7 11.2 %collective-permute-start.8 = (f32[4,136,128]{2,1,0:T(8,128)S(1)}, f32[4,136,128]{2,1,0:T(8,128)S(1)}, u32[]{:S(2)}, u32[]{:S(2)}) collective-permute-start(f32[4,136,128]{2,1,0:T(8,128)S(1)} %get-tuple-element.27), channel_id=1, source_target_pairs={{0,2},{1,3},{2,0},{3,1},{4,6},{5,7},{6,4},{7,5},{8,10},{9,11},{10,... | collective-permute-start | bytes 835592 | tf_op jit(solution)/shard_map/ppermute | solution.py:405
  29.9 11.1 %collective-permute-start.5 = (f32[128,128]{1,0:T(8,128)S(1)}, f32[128,128]{1,0:T(8,128)S(1)}, u32[]{:S(2)}, u32[]{:S(2)}) collective-permute-start(f32[128,128]{1,0:T(8,128)S(1)} %get-tuple-element.42), channel_id=1, source_target_pairs={{0,2},{1,3},{2,0},{3,1},{4,6},{5,7},{6,4},{7,5},{8,10},{9,11},{10,... | collective-permute-start | bytes 196616 | tf_op jit(solution)/shard_map/ppermute | solution.py:405
  33.8 8.2 %collective-permute-start.4 = (f32[128,128]{1,0:T(8,128)S(1)}, f32[128,128]{1,0:T(8,128)S(1)}, u32[]{:S(2)}, u32[]{:S(2)}) collective-permute-start(f32[128,128]{1,0:T(8,128)S(1)} %get-tuple-element.43), channel_id=1, source_target_pairs={{0,3},{1,0},{2,1},{3,2},{4,7},{5,4},{6,5},{7,6},{8,11},{9,8},{10,9... | collective-permute-start | bytes 196616 | tf_op jit(solution)/shard_map/ppermute | solution.py:405
  34.5 7.5 %collective-permute-start.3 = (f32[128,128]{1,0:T(8,128)S(1)}, f32[128,128]{1,0:T(8,128)S(1)}, u32[]{:S(2)}, u32[]{:S(2)}) collective-permute-start(f32[128,128]{1,0:T(8,128)S(1)} %get-tuple-element.44), channel_id=1, source_target_pairs={{0,1},{1,2},{2,3},{3,0},{4,5},{5,6},{6,7},{7,4},{8,9},{9,10},{10,1... | collective-permute-start | bytes 196616 | tf_op jit(solution)/shard_map/ppermute | solution.py:405
  37.0 6.0 %collective-permute-start.11 = (f32[136,128]{1,0:T(8,128)S(1)}, f32[136,128]{1,0:T(8,128)S(1)}, u32[]{:S(2)}, u32[]{:S(2)}) collective-permute-start(f32[136,128]{1,0:T(8,128)S(1)} %get-tuple-element.38), channel_id=1, source_target_pairs={{0,8},{1,9},{2,10},{3,11},{4,12},{5,13},{6,14},{7,15},{8,0},{9,1},... | collective-permute-start | bytes 208904 | tf_op jit(solution)/shard_map/ppermute | solution.py:402
  38.2 4.8 %collective-permute-start.10 = (f32[136,128]{1,0:T(8,128)S(1)}, f32[136,128]{1,0:T(8,128)S(1)}, u32[]{:S(2)}, u32[]{:S(2)}) collective-permute-start(f32[136,128]{1,0:T(8,128)S(1)} %get-tuple-element.39), channel_id=1, source_target_pairs={{0,12},{1,13},{2,14},{3,15},{4,0},{5,1},{6,2},{7,3},{8,4},{9,5},{1... | collective-permute-start | bytes 208904 | tf_op jit(solution)/shard_map/ppermute | solution.py:402
  40.9 5.5 %collective-permute-start.9 = (f32[136,128]{1,0:T(8,128)S(1)}, f32[136,128]{1,0:T(8,128)S(1)}, u32[]{:S(2)}, u32[]{:S(2)}) collective-permute-start(f32[136,128]{1,0:T(8,128)S(1)} %get-tuple-element.40), channel_id=1, source_target_pairs={{0,4},{1,5},{2,6},{3,7},{4,8},{5,9},{6,10},{7,11},{8,12},{9,13},{1... | collective-permute-start | bytes 208904 | tf_op jit(solution)/shard_map/ppermute | solution.py:402
  47.8 18.1 %all-to-all-start = ((f32[16,128,128]{2,1,0:T(8,128)}), f32[16,128,128]{2,1,0:T(8,128)S(1)}, u32[]{:S(2)}, u32[]{:S(2)}) async-start(f32[16,128,128]{2,1,0:T(8,128)} %get-tuple-element.35), calls=%async_computation | async-start | bytes 2097152 | tf_op jit(solution)/shard_map/all_to_all | solution.py:439
  53.6 1.4 %collective-permute-start.12 = (f32[4,32,256]{2,1,0:T(8,128)S(1)}, f32[4,32,256]{2,1,0:T(8,128)S(1)}, u32[]{:S(2)}, u32[]{:S(2)}) collective-permute-start(f32[4,32,256]{2,1,0:T(8,128)S(1)} %get-tuple-element.30), channel_id=1, source_target_pairs={{0,16},{16,0},{32,48},{48,32},{64,80},{80,64},{96,112},{112,96},{1... | collective-permute-start | bytes 393224 | tf_op jit(solution)/shard_map/ppermute | solution.py:318
  55.0 5.9 %collective-permute-start.13 = (f32[32,256]{1,0:T(8,128)S(1)}, f32[32,256]{1,0:T(8,128)S(1)}, u32[]{:S(2)}, u32[]{:S(2)}) collective-permute-start(f32[32,256]{1,0:T(8,128)S(1)} %get-tuple-element.32), channel_id=1, source_target_pairs={{0,32},{16,48},{32,64},{48,80},{64,96},{80,112},{96,0},{112,16},{1... | collective-permute-start | bytes 98312 | tf_op jit(solution)/shard_map/ppermute | solution.py:328
  56.7 5.4 %collective-permute-start.14 = (f32[32,256]{1,0:T(8,128)S(1)}, f32[32,256]{1,0:T(8,128)S(1)}, u32[]{:S(2)}, u32[]{:S(2)}) collective-permute-start(f32[32,256]{1,0:T(8,128)S(1)} %get-tuple-element.33), channel_id=1, source_target_pairs={{0,64},{16,80},{32,96},{48,112},{64,0},{80,16},{96,32},{112,48},{1... | collective-permute-start | bytes 98312 | tf_op jit(solution)/shard_map/ppermute | solution.py:328
  59.6 3.9 %collective-permute-start.15 = (f32[32,256]{1,0:T(8,128)S(1)}, f32[32,256]{1,0:T(8,128)S(1)}, u32[]{:S(2)}, u32[]{:S(2)}) collective-permute-start(f32[32,256]{1,0:T(8,128)S(1)} %get-tuple-element.34), channel_id=1, source_target_pairs={{0,96},{16,112},{32,0},{48,16},{64,32},{80,48},{96,64},{112,80},{1... | collective-permute-start | bytes 98312 | tf_op jit(solution)/shard_map/ppermute | solution.py:328
